TPU v7x, 128 devices: a whole 4x4x4 slice. The times are simulated.
128 devices in a mesh: rows: 8 (over z, y_hi), snaps: 16 (over x, y_lo, core).
Axes of the slice: x: 4, y: 4 (y_hi: 2, y_lo: 2; y = y_hi * 2 + y_lo), z: 4, core: 2. Of those that a mesh axis runs over, the one named last changes fastest.
Arguments:
- snapshots: float32 [16384, 4096], P('rows', 'snaps'), may hold values from -6 to 6
- weights: float32 [16384], P('rows'), may hold values from 0.3 to 3
- next_bricks: float32 [16384, 4096], P(('rows', 'snaps')), may hold values from -6 to 6
- brick_source: int32 [8, 64], P('rows'), may hold values from 0 to 63, each once within a row
Outputs:
- gram: float32 [4096, 4096], P('rows', 'snaps')
- next_tiles: float32 [16384, 4096], P('rows', 'snaps')
Inputs may be any that keep to these rules, and one draw needn't show every extreme that they name: Each row of brick_source is a permutation of 0 to 63.
All inputs are finite; a program needn't handle non-finite values.
Results may differ from a plain program's by a relative error of at most 0.00007.
Values sent between devices are 32-bit elements; how exact they have to be, the bound alone decides.
A program may use at most 128 MiB of HBM per device.

v0:
```python
import math

import jax
import jax.numpy as jnp
from jax import lax
from jax.sharding import Mesh
from jax.sharding import PartitionSpec as P

BRICK = 32
ROWS = ("rows_0", "rows_1")
ROWS_SNAPS = ("rows_0", "rows_1", "snaps")


def scatter_axes(x, axes, dim):
    if not axes:
        return x
    nearer = lax.psum_scatter(x, axes[0], scatter_dimension=dim, tiled=True)
    return scatter_axes(nearer, axes[1:], dim)


def pair_tile(left, right):
    return lax.dot_general(
        left,
        right,
        (((0,), (0,)), ((), ())),
        precision=lax.Precision.HIGHEST,
        preferred_element_type=jnp.float32,
    )


def per_device(snapshots, weights, next_bricks, brick_source):
    width = snapshots.shape[1]
    rows_here = snapshots.shape[0]
    weighted = snapshots * weights[:, None]
    scale = jnp.float32(math.sqrt(rows_here * lax.axis_size(ROWS)))
    column = pair_tile(lax.all_gather(snapshots, "snaps", axis=1, tiled=True), weighted)
    arrived = lax.all_to_all(next_bricks, "snaps", split_axis=1, concat_axis=0, tiled=True)
    bricks = arrived.reshape(-1, BRICK, width)
    next_tiles = jnp.take(bricks, brick_source[0], axis=0).reshape(-1, width)
    summed = scatter_axes(column, ROWS, 0)
    return (summed / scale, next_tiles)


def solution(mesh):
    torus = Mesh(mesh.devices.reshape(4, 2, mesh.shape["snaps"]), ("rows_0", "rows_1", "snaps"))
    in_specs = (P(ROWS, "snaps"), P(ROWS), P(ROWS_SNAPS, None), P(ROWS, None))
    out_specs = (P(ROWS, "snaps"), P(ROWS, "snaps"))
    return jax.shard_map(
        per_device, mesh=torus, in_specs=in_specs, out_specs=out_specs, check_vma=False
    )
```

profile of v0, /device:TPU:6, one launch (start us, length us, event | category | flops | bytes accessed | tf_op | source)
XLA Modules:
  0.0 299.8 jit_solution(7561188030469283432)
XLA Ops:
  7.2 0.0 copy-start
  7.2 0.0 all-gather.2.cloned.1.call-start
  7.2 0.7 all-gather.2.cloned.1.call-update
  7.9 0.0 reduce-scatter.3.cloned.1.call-start
  8.0 174.2 %all-gather.2.cloned.1.call-done = f32[2048,4096]{1,0:T(8,128)} async-done(((f32[2048,256]{1,0:T(8,128)}), f32[2048,4096]{1,0:T(8,128)}) %all-gather.2.cloned.1.call-update) | async-done | bytes 33554448 | tf_op jit(solution)/shard_map/all_gather | solution.py:36
  182.2 0.0 copy-done
  182.2 34.3 %convolution_bitcast_fusion = f32[4096,256]{0,1:T(8,128)} fusion(f32[2048,4096]{1,0:T(8,128)} %all-gather.2.cloned.1.call-done, f32[2048,256]{1,0:T(8,128)S(1)} %copy-done, f32[2048]{0:T(1024)} %param.5), kind=kOutput, calls=%fused_computation.1 | convolution fusion | flops 25770328064 | bytes 39854080 | tf_op jit(solution)/shard_map/dot_general | solution.py:22
  216.5 0.0 copy-start.1
  216.5 0.0 reduce-scatter.3.cloned.1.call-update
  216.5 1.6 copy-done.1
  218.1 1.8 copy.8
  219.9 0.0 copy-start.2
  219.9 5.9 %all-to-all-start = ((f32[128,16,256]{0,2,1:T(8,128)}), f32[128,16,256]{0,2,1:T(8,128)S(1)}, u32[]{:S(2)}, u32[]{:S(2)}) async-start(f32[128,16,256]{0,2,1:T(8,128)} %bitcast.15), calls=%async_computation.2 | async-start | bytes 4194304 | tf_op jit(solution)/shard_map/all_to_all | solution.py:37
  225.8 0.0 reduce-scatter.5.cloned.1.call-start
  225.9 38.9 %reduce-scatter.3.cloned.1.call-done = f32[1024,256]{0,1:T(8,128)} async-done(((f32[4096,256]{0,1:T(8,128)}), f32[1024,256]{0,1:T(8,128)}) %reduce-scatter.3.cloned.1.call-update) | async-done | bytes 1048592 | tf_op jit(solution)/shard_map/reduce_scatter | solution.py:17
  264.8 0.0 reduce-scatter.5.cloned.1.call-update
  264.8 0.0 copy-done.2
  264.8 0.1 broadcast_in_dim.15
  264.9 0.1 broadcast_in_dim.16
  265.0 0.0 all-to-all-done
  265.0 1.8 copy.9
  266.8 2.3 gather_fusion
  269.1 1.7 bitcast_select_fusion
  270.8 20.4 %reduce-scatter.5.cloned.1.call-done = f32[512,256]{0,1:T(8,128)} async-done(((f32[1024,256]{0,1:T(8,128)}), f32[512,256]{0,1:T(8,128)}) %reduce-scatter.5.cloned.1.call-update) | async-done | bytes 524304 | tf_op jit(solution)/shard_map/reduce_scatter | solution.py:17
  291.2 1.1 broadcast_multiply_fusion
  292.3 1.0 copy.10
  (3 shorter events, 0.0 us)
Async XLA Ops:
  7.2 175.0 %copy-start = (f32[2048,256]{1,0:T(8,128)S(1)}, f32[2048,256]{1,0:T(8,128)}, u32[]{:S(2)}) copy-start(f32[2048,256]{1,0:T(8,128)} %param.4) | copy-start | bytes 6291460
  7.2 175.0 %all-gather.2.cloned.1.call-start = ((), (), s32[]{:S(2)}) async-start(), calls=%async_computation.3 | async-start | bytes 35651584 | tf_op jit(solution)/shard_map/all_gather | solution.py:36
  7.9 256.9 %reduce-scatter.3.cloned.1.call-start = ((), (), s32[]{:S(2)}) async-start(), calls=%async_computation.4 | async-start | bytes 5242880 | tf_op jit(solution)/shard_map/reduce_scatter | solution.py:17
  216.5 1.6 copy-start.1
  219.9 44.9 %copy-start.2 = (s32[1,64]{1,0:T(1,128)S(1)}, s32[1,64]{1,0:T(1,128)}, u32[]{:S(2)}) copy-start(s32[1,64]{1,0:T(1,128)} %param.7) | copy-start | bytes 772
  219.9 45.1 %all-to-all-start = ((f32[128,16,256]{0,2,1:T(8,128)}), f32[128,16,256]{0,2,1:T(8,128)S(1)}, u32[]{:S(2)}, u32[]{:S(2)}) async-start(f32[128,16,256]{0,2,1:T(8,128)} %bitcast.15), calls=%async_computation.2 | async-start | bytes 4194304 | tf_op jit(solution)/shard_map/all_to_all | solution.py:37
  225.8 65.4 %reduce-scatter.5.cloned.1.call-start = ((), (), s32[]{:S(2)}) async-start(), calls=%async_computation.5 | async-start | bytes 1572864 | tf_op jit(solution)/shard_map/reduce_scatter | solution.py:17
Sparse Core Ops, SparseCore 0:
  9.6 172.4 all-gather.1
  216.6 48.0 reduce-scatter.2
  267.1 24.0 reduce-scatter.4
where the time goes:
time: 301 us; the launch traced here: 300 us
  waiting for transfers between devices  234 us (78%)
  matrix products  34.3 us (11%)
  between operations  13.8 us (5%)
  local copies, waits for them, and re-layouts  8.62 us (3%)
  starting transfers between devices  6.04 us (2%)
    all_gather x1, waiting for transfers between devices, per_device(): lax.all_gather(snapshots, 'snaps', axis=1, tiled=True)  174 us
    reduce_scatter x2, waiting for transfers between devices, scatter_axes(): nearer = lax.psum_scatter(x, axes[0], scatter_dimension=dim, tiled=True)  59.3 us
    dot_general x1, matrix products, pair_tile(): lax.dot_general(left, right, (((0,), (0,)), ((), ())), precision=lax.Prec...  34.3 us
  transfers between devices with their start and end apart: 4, of which 3 were waited for; matrix products, arithmetic and copies ran while one was open for 3% of the time, Pallas kernels for 0%

commit v1 on v0

v1 whole, which is shorter than its diff:
```python
import functools
import math

import jax
import jax.numpy as jnp
from jax import lax
from jax.experimental import pallas as pl
from jax.experimental.pallas import tpu as pltpu
from jax.sharding import PartitionSpec as P

BRICK = 32
NX, NZ = 4, 4
CHUNKS = 8
LANES = 128
LAG = 5
MESH = pl.DeviceIdType.MESH


def kernel(
    scale, snap, w_ref, bricks, gram, landed,
    xs, ahi, alo, bhi, blo, ps, zp, zm, ys,
    sem_a, sem_x, sem_h, sem_s, sem_p, sem_m, sem_y, sem_b,
    out_a, out_x, out_h, out_s, out_p, out_m, out_y, out_b,
):
    rb, me = lax.axis_index("rows"), lax.axis_index("snaps")
    z, y_hi = rb // 2, rb % 2
    x, y_lo, c = me // 4, (me // 2) % 2, me % 2
    y = y_hi * 2 + y_lo
    quarter = y_lo * 2 + c
    depth = xs.shape[3]
    half = depth // 2

    def snap_of(xx, yl, cc):
        return xx * 4 + yl * 2 + cc

    right = (rb, snap_of((x + 1) % NX, y_lo, c))
    left = (rb, snap_of((x + 3) % NX, y_lo, c))
    twin = (rb, snap_of(x, y_lo, 1 - c))
    up = (((z + 1) % NZ) * 2 + y_hi, me)
    down = (((z + 3) % NZ) * 2 + y_hi, me)

    def send(src, dst, s_sem, r_sem, to):
        return pltpu.make_async_remote_copy(
            src_ref=src, dst_ref=dst, send_sem=s_sem, recv_sem=r_sem, device_id=to, device_id_type=MESH
        )

    def arrived(dst, sem):
        pltpu.make_async_copy(dst, dst, sem).wait()

    barrier = pltpu.get_barrier_semaphore()
    for o in range(1, 16):
        pl.semaphore_signal(barrier, inc=1, device_id=(rb, (me + o) % 16), device_id_type=MESH)
    pl.semaphore_signal(barrier, inc=1, device_id=up, device_id_type=MESH)
    pl.semaphore_signal(barrier, inc=1, device_id=down, device_id_type=MESH)
    for yl in range(2):
        far = (z * 2 + 1 - y_hi, snap_of(x, yl, c))
        pl.semaphore_signal(barrier, inc=1, device_id=far, device_id_type=MESH)
    pl.semaphore_wait(barrier, 19)

    def reshard(o, part):
        q2 = (quarter + o) % 4
        k = part * 4 + c * 2 + y_lo
        src = snap.at[pl.ds(pl.multiple_of(q2 * depth, depth), depth), pl.ds(part * LANES, LANES)]
        dst = xs.at[q2 % 2, 0, k]
        if o == 0:
            return pltpu.make_async_copy(src, dst, sem_a.at[k])
        to = (rb, snap_of(x, q2 // 2, q2 % 2))
        return send(src, dst, out_a.at[o - 1, part], sem_a.at[k], to)

    def brick(o):
        s2 = (me + o) % 16
        src = bricks.at[:, pl.ds(pl.multiple_of(s2 * landed.shape[1], LANES), landed.shape[1])]
        rows = bricks.shape[0]
        dst = landed.at[pl.ds(pl.multiple_of(me * rows, rows), rows), :]
        if o == 0:
            return pltpu.make_async_copy(src, dst, sem_b.at[me])
        return send(src, dst, out_b.at[o - 1], sem_b.at[me], (rb, s2))

    for part in range(2):
        for o in range(4):
            reshard(o, part).start()
    for o in range(16):
        brick(o).start()

    def first_hop(k):
        return (
            send(xs.at[c, 0, k], xs.at[c, 3, k], out_x.at[0, k], sem_x.at[0, k], right),
            send(xs.at[c, 0, k], xs.at[c, 1, k], out_x.at[1, k], sem_x.at[1, k], left),
        )

    def first_share(k):
        return (send(xs.at[c, 0, k], xs.at[c, 0, k], out_s.at[0, k], sem_s.at[0, k], twin),)

    def second_hop(k):
        lo_rows, hi_rows = pl.ds(0, half), pl.ds(half, half)
        return (
            send(xs.at[c, 3, k, lo_rows], xs.at[c, 2, k, lo_rows], out_h.at[0, k], sem_h.at[0, k], right),
            send(xs.at[c, 1, k, hi_rows], xs.at[c, 2, k, hi_rows], out_h.at[1, k], sem_h.at[1, k], left),
            send(xs.at[c, 3, k], xs.at[c, 3, k], out_s.at[3, k], sem_s.at[3, k], twin),
            send(xs.at[c, 1, k], xs.at[c, 1, k], out_s.at[1, k], sem_s.at[1, k], twin),
        )

    def last_share(k):
        return (send(xs.at[c, 2, k], xs.at[c, 2, k], out_s.at[2, k], sem_s.at[2, k], twin),)

    own = ps.shape[2]
    top, bottom = pl.ds(0, own // 2), pl.ds(own // 2, own // 2)

    def slot_of(j):
        return (j - x + 2 * NX) % NX

    def hop(h, k):
        dp, dm = slot_of(z - h), slot_of(z + h)
        return (
            send(ps.at[k, dp, top], zp.at[k, h - 1], out_p.at[k, h - 1], sem_p.at[k, h - 1], up),
            send(ps.at[k, dm, bottom], zm.at[k, h - 1], out_m.at[k, h - 1], sem_m.at[k, h - 1], down),
        )

    def add_in(h, k):
        dp, dm = slot_of(z - h), slot_of(z + h)
        arrived(zp.at[k, h - 2], sem_p.at[k, h - 2])
        ps[k, dp, top] = ps[k, dp, top] + zp[k, h - 2]
        arrived(zm.at[k, h - 2], sem_m.at[k, h - 2])
        ps[k, dm, bottom] = ps[k, dm, bottom] + zm[k, h - 2]

    def y_send(b, k):
        yr = (k % 2) * 2 + b
        slot = (y - yr + 8) % 4 - 1
        rows = top if b == 0 else bottom
        to = (z * 2 + k % 2, snap_of(x, b, c))
        return yr, send(
            ps.at[k, slot_of(z), rows], ys.at[k // 2, slot], out_y.at[b, k], sem_y.at[k // 2, slot], to
        )

    def issue(copies):
        for copy in copies:
            copy.start()

    def own_operand():
        for yl in range(2):
            for part in range(2):
                k = part * 4 + c * 2 + yl
                for s in range(2):
                    w = w_ref[:, pl.ds(pl.multiple_of(y_lo * 2 * depth + s * depth, LANES), depth)]
                    block = xs[s, 0, k].T * (w * scale)
                    hi = block.astype(jnp.bfloat16)
                    rows = pl.ds((yl * 2 + part) * LANES, LANES)
                    cols = pl.ds(s * depth, depth)
                    ahi[rows, cols] = hi
                    alo[rows, cols] = (block - hi.astype(jnp.float32)).astype(jnp.bfloat16)

    def split(d, k, at):
        for s in range(2):
            block = xs[s, d, k]
            hi = block.astype(jnp.bfloat16)
            rows, cols = pl.ds(s * depth, depth), pl.ds(at, LANES)
            bhi[rows, cols] = hi
            blo[rows, cols] = (block - hi.astype(jnp.float32)).astype(jnp.bfloat16)

    def product(at, n):
        cols = pl.ds(at, n)
        dot = functools.partial(jnp.dot, preferred_element_type=jnp.float32)
        a, b = ahi[...], bhi[:, cols]
        return dot(a, b) + (dot(a, blo[:, cols]) + dot(alo[...], b))

    def step(i, carry):
        @pl.when(i >= 5)
        def _():
            k = i - 5

            @pl.when(y_hi == k % 2)
            def _():
                for slot in range(3):
                    arrived(ys.at[k // 2, slot], sem_y.at[k // 2, slot])
                mine = ps[k, slot_of(z), pl.ds(pl.multiple_of(y_lo * (own // 2), own // 2), own // 2)]
                total = mine + (ys[k // 2, 0] + (ys[k // 2, 1] + ys[k // 2, 2]))
                at = ((k // 2) % 2) * 256 + (k // 4) * LANES
                gram[pl.ds(pl.multiple_of(at, LANES), LANES), :] = total.T

        @pl.when((i >= 4) & (i < CHUNKS + 4))
        def _():
            k = i - 4
            add_in(4, k)
            for b in range(2):
                yr, copy = y_send(b, k)

                @pl.when(y != yr)
                def _():
                    copy.start()

        for h in (3, 2):
            @pl.when((i >= h) & (i < CHUNKS + h))
            def _():
                add_in(h, i - h)
                issue(hop(h, i - h))

        @pl.when(i + 2 < CHUNKS)
        def _():
            issue(first_hop(i + 2))

        @pl.when(i < CHUNKS)
        def _():
            arrived(xs.at[c, 3, i], sem_x.at[0, i])
            arrived(xs.at[c, 1, i], sem_x.at[1, i])
            issue(second_hop(i))

        @pl.when((i >= 1) & (i < CHUNKS + 1))
        def _():
            k = i - 1
            arrived(xs.at[c, 2, k, pl.ds(0, half)], sem_h.at[0, k])
            arrived(xs.at[c, 2, k, pl.ds(half, half)], sem_h.at[1, k])
            issue(last_share(k))
            for n, d in enumerate((0, 1, 3)):
                if d:
                    arrived(xs.at[1 - c, d, k], sem_s.at[d, k])
                split(d, k, n * LANES)
            out = product(0, 3 * LANES)
            for n, d in enumerate((0, 1, 3)):
                ps[k, d] = out[:, n * LANES : (n + 1) * LANES]
            arrived(xs.at[1 - c, 2, k], sem_s.at[2, k])
            split(2, k, 3 * LANES)
            ps[k, 2] = product(3 * LANES, LANES)
            issue(hop(1, k))

        return carry

    for k in range(CHUNKS):
        arrived(xs.at[c, 0, k], sem_a.at[k])
        issue(first_share(k))
        if k < 2:
            issue(first_hop(k))
    for k in range(CHUNKS):
        arrived(xs.at[1 - c, 0, k], sem_s.at[0, k])
    own_operand()
    lax.fori_loop(0, CHUNKS + LAG, step, 0)

    for s in range(16):
        rows = bricks.shape[0]
        arrived(landed.at[pl.ds(s * rows, rows), :], sem_b.at[s])

    for part in range(2):
        for o in range(1, 4):
            reshard(o, part).wait_send()
    for o in range(1, 16):
        brick(o).wait_send()

    def drain(k, carry):
        for copy in (*first_hop(k), *first_share(k), *second_hop(k), *last_share(k), *hop(1, k), *hop(2, k), *hop(3, k)):
            copy.wait_send()
        for b in range(2):
            yr, copy = y_send(b, k)

            @pl.when(y != yr)
            def _():
                copy.wait_send()

        return carry

    lax.fori_loop(0, CHUNKS, drain, 0)


def place(order, landed, tiles, held, sem_in, sem_out):
    def moves(q):
        there = pl.ds(pl.multiple_of(order[0, q] * BRICK, BRICK), BRICK)
        here = pl.ds(pl.multiple_of(q * BRICK, BRICK), BRICK)
        return (
            pltpu.make_async_copy(landed.at[there], held.at[q], sem_in.at[q]),
            pltpu.make_async_copy(held.at[q], tiles.at[here], sem_out.at[q]),
        )

    count = held.shape[0]
    for q in range(count):
        moves(q)[0].start()
    for q in range(count):
        into, out = moves(q)
        into.wait()
        out.start()
    for q in range(count):
        moves(q)[1].wait()


def per_device(snapshots, weights, next_bricks, brick_source):
    rows, width = snapshots.shape
    depth, own = rows // 4, 2 * width
    scale = 1.0 / math.sqrt(rows * lax.axis_size("rows"))
    f32, bf16, dma = jnp.float32, jnp.bfloat16, pltpu.SemaphoreType.DMA
    vmem = pltpu.VMEM
    space = lambda kind: pl.BlockSpec(memory_space=kind)
    gram, landed = pl.pallas_call(
        functools.partial(kernel, scale),
        out_shape=(
            jax.ShapeDtypeStruct((2 * width, width), f32),
            jax.ShapeDtypeStruct((rows, width), f32),
        ),
        in_specs=[space(pl.ANY), space(vmem), space(pl.ANY)],
        out_specs=(space(vmem), space(pl.ANY)),
        scratch_shapes=[
            vmem((2, 4, CHUNKS, depth, LANES), f32),
            vmem((own, 2 * depth), bf16),
            vmem((own, 2 * depth), bf16),
            vmem((2 * depth, 4 * LANES), bf16),
            vmem((2 * depth, 4 * LANES), bf16),
            vmem((CHUNKS, 4, own, LANES), f32),
            vmem((CHUNKS, 3, own // 2, LANES), f32),
            vmem((CHUNKS, 3, own // 2, LANES), f32),
            vmem((CHUNKS // 2, 3, own // 2, LANES), f32),
            dma((CHUNKS,)), dma((2, CHUNKS)), dma((2, CHUNKS)), dma((4, CHUNKS)),
            dma((CHUNKS, 3)), dma((CHUNKS, 3)), dma((CHUNKS // 2, 3)), dma((16,)),
            dma((3, 2)), dma((2, CHUNKS)), dma((2, CHUNKS)), dma((4, CHUNKS)),
            dma((CHUNKS, 3)), dma((CHUNKS, 3)), dma((2, CHUNKS)), dma((15,)),
        ],
        compiler_params=pltpu.CompilerParams(
            collective_id=0, has_side_effects=True, vmem_limit_bytes=60 * 1024 * 1024
        ),
    )(snapshots, weights.reshape(1, rows), next_bricks)
    count = rows // BRICK
    tiles = pl.pallas_call(
        place,
        out_shape=jax.ShapeDtypeStruct((rows, width), f32),
        in_specs=[space(pltpu.SMEM), space(pl.ANY)],
        out_specs=space(pl.ANY),
        scratch_shapes=[vmem((count, BRICK, width), f32), dma((count,)), dma((count,))],
    )(brick_source, landed)
    return gram, tiles


def solution(mesh):
    return jax.shard_map(
        per_device,
        mesh=mesh,
        in_specs=(P("rows", "snaps"), P("rows"), P(("rows", "snaps"), None), P("rows", None)),
        out_specs=(P("rows", "snaps"), P("rows", "snaps")),
        check_vma=False,
    )
```

time: 301 us -> 172 us (0.57)
  waiting for transfers between devices: 234 us -> 0 us
  Pallas kernels: 0 us -> 168 us
  matrix products: 34.3 us -> 0 us
  between operations: 13.8 us -> 0.66 us
  local copies, waits for them, and re-layouts: 8.62 us -> 0.8 us
  starting transfers between devices: 6.04 us -> 0 us
    all_gather x1 -> x0, waiting for transfers between devices: 174 us -> none  [per_device(): lax.all_gather(snapshots, 'snaps', axis=1, tiled=True)]
    pallas_call x0 -> x2, Pallas kernels: none -> 168 us  [the longest x1 164 us: per_device(): pl.pallas_call(functools.partial(kernel, scale), out_shape=(jax.ShapeDtyp...]
    reduce_scatter x2 -> x0, waiting for transfers between devices: 59.3 us -> none  [scatter_axes(): nearer = lax.psum_scatter(x, axes[0], scatter_dimension=dim, tiled=True)]
    dot_general x1 -> x0, matrix products: 34.3 us -> none  [pair_tile(): lax.dot_general(left, right, (((0,), (0,)), ((), ())), precision=lax.Prec...]
    all_to_all x1 -> x0, starting transfers between devices: 5.92 us -> none  [per_device(): lax.all_to_all(next_bricks, 'snaps', split_axis=1, concat_axis=0, tiled=T...]
    unnamed x8 -> x3, local copies, waits for them, and re-layouts: 4.37 us -> 0.8 us
  transfers between devices with their start and end apart: 4 -> 0, of which waited for: 3 -> 0; matrix products, arithmetic and copies ran while one was open for 3% -> 0% of each run, Pallas kernels for 0% -> 0%
where the time goes in v1:
time: 172 us; the launch traced here: 169 us
  Pallas kernels  168 us (98%)
    pallas_call x1, Pallas kernels, per_device(): pl.pallas_call(functools.partial(kernel, scale), out_shape=(jax.ShapeDtyp...  164 us
    pallas_call x1, Pallas kernels, per_device(): pl.pallas_call(place, out_shape=jax.ShapeDtypeStruct((rows, width), f32),...  4.07 us

profile of v1, /device:TPU:6, one launch (start us, length us, event | category | flops | bytes accessed | tf_op | source)
XLA Modules:
  0.0 169.2 jit_solution(7258621376989080315)
XLA Ops:
  0.6 163.7 %shard_map.59 = (f32[512,256]{1,0:T(8,128)}, f32[2048,256]{1,0:T(8,128)}) custom-call(f32[2048,256]{1,0:T(8,128)} %snap.1, f32[1,2048]{1,0:T(1,128)} %bitcast.1, f32[128,4096]{1,0:T(8,128)} %bricks.1), custom_call_target="tpu_custom_call" | custom-call | tf_op jit(solution)/shard_map/pallas_call | solution.py:289
  164.3 0.0 copy-start
  164.3 4.1 %shard_map.60 = f32[2048,256]{1,0:T(8,128)} custom-call(s32[1,64]{1,0:T(1,128)} %order.1, f32[2048,256]{1,0:T(8,128)} %get-tuple-element.5.landed), custom_call_target="tpu_custom_call" | custom-call | tf_op jit(solution)/shard_map/pallas_call | solution.py:317
  168.4 0.0 copy-done
  168.4 0.8 copy.7
Async XLA Ops:
  164.3 4.1 %copy-start = (f32[512,256]{1,0:T(8,128)S(1)}, f32[512,256]{1,0:T(8,128)}, u32[]{:S(2)}) copy-start(f32[512,256]{1,0:T(8,128)} %get-tuple-element.8) | copy-start | bytes 1572868

commit v2 on v1

--- a/solution.py
+++ b/solution.py
@@ -12,15 +12,15 @@
 NX, NZ = 4, 4
 CHUNKS = 8
 LANES = 128
-LAG = 5
+LAG = 4
 MESH = pl.DeviceIdType.MESH
 
 
 def kernel(
     scale, snap, w_ref, bricks, gram, landed,
-    xs, ahi, alo, bhi, blo, ps, zp, zm, ys,
-    sem_a, sem_x, sem_h, sem_s, sem_p, sem_m, sem_y, sem_b,
-    out_a, out_x, out_h, out_s, out_p, out_m, out_y, out_b,
+    xs, ahi, alo, bhi, blo, ps, zs, ys,
+    sem_a, sem_x, sem_h, sem_s, sem_z, sem_y, sem_b,
+    out_a, out_x, out_h, out_s, out_z, out_y, out_b,
 ):
     rb, me = lax.axis_index("rows"), lax.axis_index("snaps")
     z, y_hi = rb // 2, rb % 2
@@ -68,11 +68,12 @@
         return send(src, dst, out_a.at[o - 1, part], sem_a.at[k], to)
 
     def brick(o):
-        s2 = (me + o) % 16
+        dx, dy, dc = o // 4, (o // 2) % 2, o % 2
+        s2 = snap_of((x + dx) % NX, (y_lo + dy) % 2, (c + dc) % 2)
         src = bricks.at[:, pl.ds(pl.multiple_of(s2 * landed.shape[1], LANES), landed.shape[1])]
         rows = bricks.shape[0]
         dst = landed.at[pl.ds(pl.multiple_of(me * rows, rows), rows), :]
-        if o == 0:
+        if isinstance(o, int) and o == 0:
             return pltpu.make_async_copy(src, dst, sem_b.at[me])
         return send(src, dst, out_b.at[o - 1], sem_b.at[me], (rb, s2))
 
@@ -80,7 +81,8 @@
         for o in range(4):
             reshard(o, part).start()
     for o in range(16):
-        brick(o).start()
+        if (o // 2) % 2 == 0:
+            brick(o).start()
 
     def first_hop(k):
         return (
@@ -109,19 +111,27 @@
     def slot_of(j):
         return (j - x + 2 * NX) % NX
 
-    def hop(h, k):
-        dp, dm = slot_of(z - h), slot_of(z + h)
+    def z_send(n, k, j, rows, to):
+        return send(ps.at[k, slot_of(j), rows], zs.at[n, k], out_z.at[n, k], sem_z.at[n, k], to)
+
+    def z_first(k):
         return (
-            send(ps.at[k, dp, top], zp.at[k, h - 1], out_p.at[k, h - 1], sem_p.at[k, h - 1], up),
-            send(ps.at[k, dm, bottom], zm.at[k, h - 1], out_m.at[k, h - 1], sem_m.at[k, h - 1], down),
-        )
-
-    def add_in(h, k):
-        dp, dm = slot_of(z - h), slot_of(z + h)
-        arrived(zp.at[k, h - 2], sem_p.at[k, h - 2])
-        ps[k, dp, top] = ps[k, dp, top] + zp[k, h - 2]
-        arrived(zm.at[k, h - 2], sem_m.at[k, h - 2])
-        ps[k, dm, bottom] = ps[k, dm, bottom] + zm[k, h - 2]
+            z_send(0, k, z + 2, top, down),
+            z_send(1, k, z + 2, bottom, up),
+            z_send(2, k, z + 1, top, up),
+            z_send(3, k, z - 1, bottom, down),
+        )
+
+    def z_second(k):
+        return (z_send(4, k, z - 1, top, down), z_send(5, k, z + 1, bottom, up))
+
+    def z_add(k, j, rows, ns):
+        d = slot_of(j)
+        total = ps[k, d, rows]
+        for n in ns:
+            arrived(zs.at[n, k], sem_z.at[n, k])
+            total = total + zs[n, k]
+        ps[k, d, rows] = total
 
     def y_send(b, k):
         yr = (k % 2) * 2 + b
@@ -164,9 +174,63 @@
         return dot(a, b) + (dot(a, blo[:, cols]) + dot(alo[...], b))
 
     def step(i, carry):
-        @pl.when(i >= 5)
-        def _():
-            k = i - 5
+        @pl.when(i < CHUNKS)
+        def _():
+            arrived(xs.at[c, 3, i], sem_x.at[0, i])
+            arrived(xs.at[c, 1, i], sem_x.at[1, i])
+            issue(second_hop(i))
+            brick((i // 2) * 4 + 2 + i % 2).start()
+
+        @pl.when(i + 4 < CHUNKS)
+        def _():
+            issue(first_hop(i + 4))
+
+        @pl.when((i >= 1) & (i < CHUNKS + 1))
+        def _():
+            arrived(xs.at[c, 2, i - 1, pl.ds(0, half)], sem_h.at[0, i - 1])
+            arrived(xs.at[c, 2, i - 1, pl.ds(half, half)], sem_h.at[1, i - 1])
+            issue(last_share(i - 1))
+
+        @pl.when(i < CHUNKS)
+        def _():
+            arrived(xs.at[1 - c, 1, i], sem_s.at[1, i])
+            arrived(xs.at[1 - c, 3, i], sem_s.at[3, i])
+            for n, d in enumerate((0, 1, 3)):
+                split(d, i, n * LANES)
+            out = product(0, 3 * LANES)
+            for n, d in enumerate((0, 1, 3)):
+                ps[i, d] = out[:, n * LANES : (n + 1) * LANES]
+
+        @pl.when((i >= 1) & (i < CHUNKS + 1))
+        def _():
+            k = i - 1
+            arrived(xs.at[1 - c, 2, k], sem_s.at[2, k])
+            split(2, k, 3 * LANES)
+            ps[k, 2] = product(3 * LANES, LANES)
+            issue(z_first(k))
+
+        @pl.when((i >= 2) & (i < CHUNKS + 2))
+        def _():
+            k = i - 2
+            z_add(k, z - 1, top, (0,))
+            z_add(k, z + 1, bottom, (1,))
+            issue(z_second(k))
+
+        @pl.when((i >= 3) & (i < CHUNKS + 3))
+        def _():
+            k = i - 3
+            z_add(k, z, top, (2, 4))
+            z_add(k, z, bottom, (3, 5))
+            for b in range(2):
+                yr, copy = y_send(b, k)
+
+                @pl.when(y != yr)
+                def _():
+                    copy.start()
+
+        @pl.when(i >= 4)
+        def _():
+            k = i - 4
 
             @pl.when(y_hi == k % 2)
             def _():
@@ -177,58 +241,16 @@
                 at = ((k // 2) % 2) * 256 + (k // 4) * LANES
                 gram[pl.ds(pl.multiple_of(at, LANES), LANES), :] = total.T
 
-        @pl.when((i >= 4) & (i < CHUNKS + 4))
-        def _():
-            k = i - 4
-            add_in(4, k)
-            for b in range(2):
-                yr, copy = y_send(b, k)
-
-                @pl.when(y != yr)
-                def _():
-                    copy.start()
-
-        for h in (3, 2):
-            @pl.when((i >= h) & (i < CHUNKS + h))
-            def _():
-                add_in(h, i - h)
-                issue(hop(h, i - h))
-
-        @pl.when(i + 2 < CHUNKS)
-        def _():
-            issue(first_hop(i + 2))
-
-        @pl.when(i < CHUNKS)
-        def _():
-            arrived(xs.at[c, 3, i], sem_x.at[0, i])
-            arrived(xs.at[c, 1, i], sem_x.at[1, i])
-            issue(second_hop(i))
-
-        @pl.when((i >= 1) & (i < CHUNKS + 1))
-        def _():
-            k = i - 1
-            arrived(xs.at[c, 2, k, pl.ds(0, half)], sem_h.at[0, k])
-            arrived(xs.at[c, 2, k, pl.ds(half, half)], sem_h.at[1, k])
-            issue(last_share(k))
-            for n, d in enumerate((0, 1, 3)):
-                if d:
-                    arrived(xs.at[1 - c, d, k], sem_s.at[d, k])
-                split(d, k, n * LANES)
-            out = product(0, 3 * LANES)
-            for n, d in enumerate((0, 1, 3)):
-                ps[k, d] = out[:, n * LANES : (n + 1) * LANES]
-            arrived(xs.at[1 - c, 2, k], sem_s.at[2, k])
-            split(2, k, 3 * LANES)
-            ps[k, 2] = product(3 * LANES, LANES)
-            issue(hop(1, k))
-
         return carry
 
-    for k in range(CHUNKS):
-        arrived(xs.at[c, 0, k], sem_a.at[k])
-        issue(first_share(k))
-        if k < 2:
-            issue(first_hop(k))
+    for part in range(2):
+        for far in range(2):
+            for cc in range(2):
+                k = part * 4 + cc * 2 + (y_lo + far) % 2
+                arrived(xs.at[c, 0, k], sem_a.at[k])
+                issue(first_share(k))
+                if part == 0:
+                    issue(first_hop(k))
     for k in range(CHUNKS):
         arrived(xs.at[1 - c, 0, k], sem_s.at[0, k])
     own_operand()
@@ -245,7 +267,7 @@
         brick(o).wait_send()
 
     def drain(k, carry):
-        for copy in (*first_hop(k), *first_share(k), *second_hop(k), *last_share(k), *hop(1, k), *hop(2, k), *hop(3, k)):
+        for copy in (*first_hop(k), *first_share(k), *second_hop(k), *last_share(k), *z_first(k), *z_second(k)):
             copy.wait_send()
         for b in range(2):
             yr, copy = y_send(b, k)
@@ -301,13 +323,12 @@
             vmem((2 * depth, 4 * LANES), bf16),
             vmem((2 * depth, 4 * LANES), bf16),
             vmem((CHUNKS, 4, own, LANES), f32),
-            vmem((CHUNKS, 3, own // 2, LANES), f32),
-            vmem((CHUNKS, 3, own // 2, LANES), f32),
+            vmem((6, CHUNKS, own // 2, LANES), f32),
             vmem((CHUNKS // 2, 3, own // 2, LANES), f32),
             dma((CHUNKS,)), dma((2, CHUNKS)), dma((2, CHUNKS)), dma((4, CHUNKS)),
-            dma((CHUNKS, 3)), dma((CHUNKS, 3)), dma((CHUNKS // 2, 3)), dma((16,)),
+            dma((6, CHUNKS)), dma((CHUNKS // 2, 3)), dma((16,)),
             dma((3, 2)), dma((2, CHUNKS)), dma((2, CHUNKS)), dma((4, CHUNKS)),
-            dma((CHUNKS, 3)), dma((CHUNKS, 3)), dma((2, CHUNKS)), dma((15,)),
+            dma((6, CHUNKS)), dma((2, CHUNKS)), dma((15,)),
         ],
         compiler_params=pltpu.CompilerParams(
             collective_id=0, has_side_effects=True, vmem_limit_bytes=60 * 1024 * 1024

time: 172 us -> 147 us (0.85)
  the two profiles are of different devices: /device:TPU:6 before, /device:TPU:1 now
where the time goes in v2:
time: 147 us; the launch traced here: 146 us
  Pallas kernels  145 us (99%)
    pallas_call x1, Pallas kernels, per_device(): pl.pallas_call(functools.partial(kernel, scale), out_shape=(jax.ShapeDtyp...  141 us
    pallas_call x1, Pallas kernels, per_device(): pl.pallas_call(place, out_shape=jax.ShapeDtypeStruct((rows, width), f32),...  4.07 us

profile of v2, /device:TPU:1, one launch (start us, length us, event | category | flops | bytes accessed | tf_op | source)
XLA Modules:
  0.0 146.4 jit_solution(2530464755955061578)
XLA Ops:
  0.6 140.9 %shard_map.59 = (f32[512,256]{1,0:T(8,128)}, f32[2048,256]{1,0:T(8,128)}) custom-call(f32[2048,256]{1,0:T(8,128)} %snap.1, f32[1,2048]{1,0:T(1,128)} %bitcast.1, f32[128,4096]{1,0:T(8,128)} %bricks.1), custom_call_target="tpu_custom_call" | custom-call | tf_op jit(solution)/shard_map/pallas_call | solution.py:311
  141.5 0.0 copy-start
  141.5 4.1 %shard_map.60 = f32[2048,256]{1,0:T(8,128)} custom-call(s32[1,64]{1,0:T(1,128)} %order.1, f32[2048,256]{1,0:T(8,128)} %get-tuple-element.5.landed), custom_call_target="tpu_custom_call" | custom-call | tf_op jit(solution)/shard_map/pallas_call | solution.py:338
  145.6 0.0 copy-done
  145.6 0.8 copy.7
Async XLA Ops:
  141.5 4.1 %copy-start = (f32[512,256]{1,0:T(8,128)S(1)}, f32[512,256]{1,0:T(8,128)}, u32[]{:S(2)}) copy-start(f32[512,256]{1,0:T(8,128)} %get-tuple-element.8) | copy-start | bytes 1572868

commit v3 on v2

v3 whole, which is shorter than its diff:
```python
import functools
import math

import jax
import jax.numpy as jnp
from jax import lax
from jax.experimental import pallas as pl
from jax.experimental.pallas import tpu as pltpu
from jax.sharding import PartitionSpec as P

BRICK = 32
NX, NZ = 4, 4
CHUNKS = 8
LANES = 128
LAG = 3
MESH = pl.DeviceIdType.MESH


def kernel(
    scale, snap, w_ref, bricks, order, gram, tiles,
    xs, ahi, alo, bhi, blo, ps, zs, ys, landed, placed,
    sem_a, sem_x, sem_h, sem_s, sem_z, sem_y, sem_b,
    out_a, out_x, out_h, out_s, out_z, out_y, out_b, out_t,
):
    rb, me = lax.axis_index("rows"), lax.axis_index("snaps")
    z, y_hi = rb // 2, rb % 2
    x, y_lo, c = me // 4, (me // 2) % 2, me % 2
    y = y_hi * 2 + y_lo
    depth = xs.shape[3]
    half = depth // 2

    def snap_of(xx, yl, cc):
        return xx * 4 + yl * 2 + cc

    right = (rb, snap_of((x + 1) % NX, y_lo, c))
    left = (rb, snap_of((x + 3) % NX, y_lo, c))
    twin = (rb, snap_of(x, y_lo, 1 - c))
    up = (((z + 1) % NZ) * 2 + y_hi, me)
    down = (((z + 3) % NZ) * 2 + y_hi, me)

    def send(src, dst, s_sem, r_sem, to):
        return pltpu.make_async_remote_copy(
            src_ref=src, dst_ref=dst, send_sem=s_sem, recv_sem=r_sem, device_id=to, device_id_type=MESH
        )

    def arrived(dst, sem):
        pltpu.make_async_copy(dst, dst, sem).wait()

    barrier = pltpu.get_barrier_semaphore()
    for o in range(1, 16):
        pl.semaphore_signal(barrier, inc=1, device_id=(rb, (me + o) % 16), device_id_type=MESH)
    pl.semaphore_signal(barrier, inc=1, device_id=up, device_id_type=MESH)
    pl.semaphore_signal(barrier, inc=1, device_id=down, device_id_type=MESH)
    for yl in range(2):
        far = (z * 2 + 1 - y_hi, snap_of(x, yl, c))
        pl.semaphore_signal(barrier, inc=1, device_id=far, device_id_type=MESH)
    pl.semaphore_wait(barrier, 19)

    def reshard(o, part):
        y2, c2 = (y_lo + o // 2) % 2, (c + o % 2) % 2
        q2 = y2 * 2 + c2
        k = (o // 2) * 4 + part * 2 + c
        src = snap.at[pl.ds(pl.multiple_of(q2 * depth, depth), depth), pl.ds(part * LANES, LANES)]
        dst = xs.at[c2, 0, k]
        if o == 0:
            return pltpu.make_async_copy(src, dst, sem_a.at[k])
        to = (rb, snap_of(x, y2, c2))
        return send(src, dst, out_a.at[o - 1, part], sem_a.at[k], to)

    def brick(o):
        dx, dy, dc = o // 4, (o // 2) % 2, o % 2
        s2 = snap_of((x + dx) % NX, (y_lo + dy) % 2, (c + dc) % 2)
        width = landed.shape[2]
        src = bricks.at[:, :, pl.ds(pl.multiple_of(s2 * width, LANES), width)]
        count = bricks.shape[0]
        dst = landed.at[pl.ds(me * count, count)]
        if isinstance(o, int) and o == 0:
            return pltpu.make_async_copy(src, dst, sem_b.at[me])
        return send(src, dst, out_b.at[o - 1], sem_b.at[me], (rb, s2))

    for part in range(2):
        for o in (0, 1, 2, 3):
            reshard(o, part).start()
    brick(0).start()
    brick(1).start()

    def first_hop(k):
        return (
            send(xs.at[c, 0, k], xs.at[c, 3, k], out_x.at[0, k], sem_x.at[0, k], right),
            send(xs.at[c, 0, k], xs.at[c, 1, k], out_x.at[1, k], sem_x.at[1, k], left),
        )

    def first_share(k):
        return (send(xs.at[c, 0, k], xs.at[c, 0, k], out_s.at[0, k], sem_s.at[0, k], twin),)

    def second_hop(k):
        lo_rows, hi_rows = pl.ds(0, half), pl.ds(half, half)
        return (
            send(xs.at[c, 3, k, lo_rows], xs.at[c, 2, k, lo_rows], out_h.at[0, k], sem_h.at[0, k], right),
            send(xs.at[c, 1, k, hi_rows], xs.at[c, 2, k, hi_rows], out_h.at[1, k], sem_h.at[1, k], left),
            send(xs.at[c, 3, k], xs.at[c, 3, k], out_s.at[3, k], sem_s.at[3, k], twin),
            send(xs.at[c, 1, k], xs.at[c, 1, k], out_s.at[1, k], sem_s.at[1, k], twin),
        )

    def last_share(k):
        return (send(xs.at[c, 2, k], xs.at[c, 2, k], out_s.at[2, k], sem_s.at[2, k], twin),)

    own = ps.shape[2]
    top, bottom = pl.ds(0, own // 2), pl.ds(own // 2, own // 2)

    def slot_of(j):
        return (j - x + 2 * NX) % NX

    def z_send(n, k, j, rows, to):
        return send(ps.at[k, slot_of(j), rows], zs.at[n, k], out_z.at[n, k], sem_z.at[n, k], to)

    def z_first(k):
        return (
            z_send(0, k, z + 2, top, down),
            z_send(1, k, z + 2, bottom, up),
            z_send(2, k, z + 1, top, up),
            z_send(3, k, z - 1, bottom, down),
        )

    def z_second(k):
        return (z_send(4, k, z - 1, top, down), z_send(5, k, z + 1, bottom, up))

    def z_add(k, j, rows, ns):
        d = slot_of(j)
        total = ps[k, d, rows]
        for n in ns:
            arrived(zs.at[n, k], sem_z.at[n, k])
            total = total + zs[n, k]
        ps[k, d, rows] = total

    def y_send(b, k):
        h, m = (y_lo + k // 4) % 2, k % 4
        yr = h * 2 + b
        slot = (y - yr + 8) % 4 - 1
        rows = top if b == 0 else bottom
        to = (z * 2 + h, snap_of(x, b, c))
        return yr, send(ps.at[k, slot_of(z), rows], ys.at[m, slot], out_y.at[b, k], sem_y.at[m, slot], to)

    def issue(copies):
        for copy in copies:
            copy.start()

    def own_operand():
        for far in range(2):
            for part in range(2):
                k = far * 4 + part * 2 + c
                at = ((y_lo + far) % 2) * 2 * LANES + part * LANES
                rows = pl.ds(pl.multiple_of(at, LANES), LANES)
                for s in range(2):
                    w = w_ref[:, pl.ds(pl.multiple_of(y_lo * 2 * depth + s * depth, LANES), depth)]
                    block = xs[s, 0, k].T * (w * scale)
                    hi = block.astype(jnp.bfloat16)
                    cols = pl.ds(s * depth, depth)
                    ahi[rows, cols] = hi
                    alo[rows, cols] = (block - hi.astype(jnp.float32)).astype(jnp.bfloat16)

    def split(d, k, at):
        for s in range(2):
            block = xs[s, d, k]
            hi = block.astype(jnp.bfloat16)
            rows, cols = pl.ds(s * depth, depth), pl.ds(at, LANES)
            bhi[rows, cols] = hi
            blo[rows, cols] = (block - hi.astype(jnp.float32)).astype(jnp.bfloat16)

    def product():
        dot = functools.partial(jnp.dot, preferred_element_type=jnp.float32)
        a, b = ahi[...], bhi[...]
        return dot(a, b) + (dot(a, blo[...]) + dot(alo[...], b))

    def pass_on(k):
        arrived(xs.at[c, 3, k], sem_x.at[0, k])
        arrived(xs.at[c, 1, k], sem_x.at[1, k])
        issue(second_hop(k))

    def pass_last(k):
        arrived(xs.at[c, 2, k, pl.ds(0, half)], sem_h.at[0, k])
        arrived(xs.at[c, 2, k, pl.ds(half, half)], sem_h.at[1, k])
        issue(last_share(k))

    def step(i, carry):
        @pl.when(i < CHUNKS)
        def _():
            for d in (1, 2, 3):
                arrived(xs.at[1 - c, d, i], sem_s.at[d, i])
            for d in range(4):
                split(d, i, d * LANES)
            out = product()
            for d in range(4):
                ps[i, d] = out[:, d * LANES : (d + 1) * LANES]
            issue(z_first(i))

        @pl.when(i + 3 < CHUNKS)
        def _():
            pass_on(i + 3)

        @pl.when(i + 5 < CHUNKS)
        def _():
            issue(first_hop(i + 5))

        @pl.when(i + 3 == CHUNKS - 1)
        def _():
            for n in range(4, 16):
                brick(n).start()

        @pl.when(i + 2 < CHUNKS)
        def _():
            pass_last(i + 2)

        @pl.when((i >= 1) & (i < CHUNKS + 1))
        def _():
            k = i - 1
            z_add(k, z - 1, top, (0,))
            z_add(k, z + 1, bottom, (1,))
            issue(z_second(k))

        @pl.when((i >= 2) & (i < CHUNKS + 2))
        def _():
            k = i - 2
            z_add(k, z, top, (2, 4))
            z_add(k, z, bottom, (3, 5))
            for b in range(2):
                yr, copy = y_send(b, k)

                @pl.when(y != yr)
                def _():
                    copy.start()

        @pl.when(i >= 4 + LAG)
        def _():
            m = i - 4 - LAG
            k = ((y_hi + y_lo) % 2) * 4 + m
            for slot in range(3):
                arrived(ys.at[m, slot], sem_y.at[m, slot])
            mine = ps[k, slot_of(z), pl.ds(pl.multiple_of(y_lo * (own // 2), own // 2), own // 2)]
            total = mine + (ys[m, 0] + (ys[m, 1] + ys[m, 2]))
            at = (m % 2) * 2 * LANES + (m // 2) * LANES
            gram[pl.ds(pl.multiple_of(at, LANES), LANES), :] = total.T

        return carry

    def ready(k):
        arrived(xs.at[c, 0, k], sem_a.at[k])
        issue(first_share(k))

    for k in range(4):
        ready(k)
        if k < 2:
            issue(first_hop(k))
    pass_on(0)
    issue(first_hop(2))
    pass_on(1)
    issue(first_hop(3))
    pass_last(0)
    ready(4)
    ready(5)
    pass_on(2)
    issue(first_hop(4))
    pass_last(1)
    ready(6)
    ready(7)
    brick(2).start()
    brick(3).start()
    for k in range(CHUNKS):
        arrived(xs.at[1 - c, 0, k], sem_s.at[0, k])
    own_operand()
    lax.fori_loop(0, CHUNKS + 1, step, 0)
    count = bricks.shape[0]
    for s in range(16):
        arrived(landed.at[pl.ds(s * count, count)], sem_b.at[s])

    def place(q, carry):
        placed[q] = landed[order[0, q]]
        return carry

    lax.fori_loop(0, placed.shape[0], place, 0)
    written = pltpu.make_async_copy(placed, tiles, out_t)
    written.start()
    lax.fori_loop(CHUNKS + 1, CHUNKS + LAG, step, 0)
    written.wait()

    for part in range(2):
        for o in range(1, 4):
            reshard(o, part).wait_send()
    for o in range(1, 16):
        brick(o).wait_send()

    def drain(k, carry):
        for copy in (*first_hop(k), *first_share(k), *second_hop(k), *last_share(k), *z_first(k), *z_second(k)):
            copy.wait_send()
        for b in range(2):
            yr, copy = y_send(b, k)

            @pl.when(y != yr)
            def _():
                copy.wait_send()

        return carry

    lax.fori_loop(0, CHUNKS, drain, 0)


def per_device(snapshots, weights, next_bricks, brick_source):
    rows, width = snapshots.shape
    depth, own = rows // 4, 2 * width
    scale = 1.0 / math.sqrt(rows * lax.axis_size("rows"))
    f32, bf16, dma = jnp.float32, jnp.bfloat16, pltpu.SemaphoreType.DMA
    vmem = pltpu.VMEM
    space = lambda kind: pl.BlockSpec(memory_space=kind)
    count = rows // BRICK
    gram, tiles = pl.pallas_call(
        functools.partial(kernel, scale),
        out_shape=(
            jax.ShapeDtypeStruct((2 * width, width), f32),
            jax.ShapeDtypeStruct((count, BRICK, width), f32),
        ),
        in_specs=[space(pl.ANY), space(vmem), space(pl.ANY), space(pltpu.SMEM)],
        out_specs=(space(vmem), space(pl.ANY)),
        scratch_shapes=[
            vmem((2, 4, CHUNKS, depth, LANES), f32),
            vmem((own, 2 * depth), bf16),
            vmem((own, 2 * depth), bf16),
            vmem((2 * depth, 4 * LANES), bf16),
            vmem((2 * depth, 4 * LANES), bf16),
            vmem((CHUNKS, 4, own, LANES), f32),
            vmem((6, CHUNKS, own // 2, LANES), f32),
            vmem((CHUNKS // 2, 3, own // 2, LANES), f32),
            vmem((count, BRICK, width), f32),
            vmem((count, BRICK, width), f32),
            dma((CHUNKS,)), dma((2, CHUNKS)), dma((2, CHUNKS)), dma((4, CHUNKS)),
            dma((6, CHUNKS)), dma((CHUNKS // 2, 3)), dma((16,)),
            dma((3, 2)), dma((2, CHUNKS)), dma((2, CHUNKS)), dma((4, CHUNKS)),
            dma((6, CHUNKS)), dma((2, CHUNKS)), dma((15,)), dma,
        ],
        compiler_params=pltpu.CompilerParams(
            collective_id=0, has_side_effects=True, vmem_limit_bytes=60 * 1024 * 1024
        ),
    )(snapshots, weights.reshape(1, rows), next_bricks.reshape(-1, BRICK, next_bricks.shape[1]), brick_source)
    return gram, tiles.reshape(rows, width)


def solution(mesh):
    return jax.shard_map(
        per_device,
        mesh=mesh,
        in_specs=(P("rows", "snaps"), P("rows"), P(("rows", "snaps"), None), P("rows", None)),
        out_specs=(P("rows", "snaps"), P("rows", "snaps")),
        check_vma=False,
    )
```

time: 147 us -> 128 us (0.87)
  the two profiles are of different devices: /device:TPU:1 before, /device:TPU:4 now
where the time goes in v3:
time: 128 us; the launch traced here: 127 us
  Pallas kernels  122 us (95%)
  local copies, waits for them, and re-layouts  4.91 us (4%)
    pallas_call x1, Pallas kernels, per_device(): pl.pallas_call(functools.partial(kernel, scale), out_shape=(jax.ShapeDtyp...  122 us
    unnamed x2, local copies, waits for them, and re-layouts  4.91 us

profile of v3, /device:TPU:4, one launch (start us, length us, event | category | flops | bytes accessed | tf_op | source)
XLA Modules:
  0.0 127.4 jit_solution(17915642644217881728)
XLA Ops:
  0.6 121.8 %shard_map.59 = (f32[512,256]{1,0:T(8,128)}, f32[64,32,256]{2,1,0:T(8,128)}) custom-call(f32[2048,256]{1,0:T(8,128)} %snap.1, f32[1,2048]{1,0:T(1,128)} %bitcast.5, f32[4,32,4096]{2,1,0:T(8,128)} %bitcast.3, s32[1,64]{1,0:T(1,128)} %order.1), custom_call_target="tpu_custom_call" | custom-call | tf_op jit(solution)/shard_map/pallas_call | solution.py:315
  122.4 1.9 %copy.8 = f32[512,256]{1,0:T(8,128)} copy(f32[512,256]{1,0:T(8,128)} %get-tuple-element.8) | data formatting | bytes 1048576
  124.3 3.0 %copy.9 = f32[2048,256]{1,0:T(8,128)} copy(f32[2048,256]{1,0:T(8,128)} %bitcast.4) | data formatting | bytes 4194304

commit v4 on v3

--- a/solution.py
+++ b/solution.py
@@ -13,14 +13,15 @@
 CHUNKS = 8
 LANES = 128
 LAG = 3
+EARLY = 2
 MESH = pl.DeviceIdType.MESH
 
 
 def kernel(
     scale, snap, w_ref, bricks, order, gram, tiles,
-    xs, ahi, alo, bhi, blo, ps, zs, ys, landed, placed,
-    sem_a, sem_x, sem_h, sem_s, sem_z, sem_y, sem_b,
-    out_a, out_x, out_h, out_s, out_z, out_y, out_b, out_t,
+    xs, ahi, alo, bhi, blo, ps, zs, ys, landed, relay, across,
+    sem_a, sem_x, sem_h, sem_s, sem_z, sem_y, sem_b, sem_r, sem_o,
+    out_a, out_x, out_h, out_s, out_z, out_y, out_b, out_r, out_o, out_n,
 ):
     rb, me = lax.axis_index("rows"), lax.axis_index("snaps")
     z, y_hi = rb // 2, rb % 2
@@ -68,15 +69,48 @@
         return send(src, dst, out_a.at[o - 1, part], sem_a.at[k], to)
 
     def brick(o):
-        dx, dy, dc = o // 4, (o // 2) % 2, o % 2
-        s2 = snap_of((x + dx) % NX, (y_lo + dy) % 2, (c + dc) % 2)
+        s2 = snap_of(x, (y_lo + o // 2) % 2, (c + o % 2) % 2)
         width = landed.shape[2]
         src = bricks.at[:, :, pl.ds(pl.multiple_of(s2 * width, LANES), width)]
         count = bricks.shape[0]
         dst = landed.at[pl.ds(me * count, count)]
-        if isinstance(o, int) and o == 0:
+        if o == 0:
             return pltpu.make_async_copy(src, dst, sem_b.at[me])
         return send(src, dst, out_b.at[o - 1], sem_b.at[me], (rb, s2))
+
+    def brick_cols(dx, dy, dc):
+        width = landed.shape[2]
+        s2 = snap_of((x + dx) % NX, (y_lo + dy) % 2, (c + dc) % 2)
+        return bricks.at[:, :, pl.ds(pl.multiple_of(s2 * width, LANES), width)]
+
+    def rows_from(source):
+        return landed.at[pl.ds(source * bricks.shape[0], bricks.shape[0])]
+
+    def brick_over(dx, dc):
+        to = (rb, snap_of(x, 1 - y_lo, c))
+        dst = across.at[dx - 1, dc]
+        return send(brick_cols(dx, 1, dc), dst, out_o.at[dx - 1, dc], sem_o.at[dx - 1, dc], to)
+
+    def held_bricks(dx, dy, dc):
+        return across.at[dx - 1, dc] if dy else brick_cols(dx, 0, dc)
+
+    def brick_near(dx, dy, dc):
+        source = snap_of(x, (y_lo + dy) % 2, c)
+        to = (rb, snap_of((x + dx) % NX, y_lo, (c + dc) % 2))
+        sem = out_n.at[dx // 2, dy, dc]
+        return send(held_bricks(dx, dy, dc), rows_from(source), sem, sem_b.at[source], to)
+
+    def brick_far(g, dy):
+        ahead, behind = (x + 1 + 2 * g) % NX, (x + 3 - 2 * g) % NX
+        source = snap_of(behind, (y_lo + dy) % 2, c)
+        to = (rb, snap_of(ahead, y_lo, (c + g) % 2))
+        hop = send(
+            held_bricks(2, dy, g), relay.at[g, dy], out_r.at[0, g, dy], sem_r.at[g, dy], left if g else right
+        )
+        return hop, send(relay.at[g, dy], rows_from(source), out_r.at[1, g, dy], sem_b.at[source], to)
+
+    near = [(dx, dy, dc) for dx in (1, 3) for dy in range(2) for dc in range(2)]
+    over = [(dx, dc) for dx in (1, 2, 3) for dc in range(2)]
 
     for part in range(2):
         for o in (0, 1, 2, 3):
@@ -114,13 +148,10 @@
     def z_send(n, k, j, rows, to):
         return send(ps.at[k, slot_of(j), rows], zs.at[n, k], out_z.at[n, k], sem_z.at[n, k], to)
 
-    def z_first(k):
-        return (
-            z_send(0, k, z + 2, top, down),
-            z_send(1, k, z + 2, bottom, up),
-            z_send(2, k, z + 1, top, up),
-            z_send(3, k, z - 1, bottom, down),
-        )
+    def z_first(k, b):
+        if b == 0:
+            return (z_send(0, k, z + 2, top, down), z_send(2, k, z + 1, top, up))
+        return (z_send(1, k, z + 2, bottom, up), z_send(3, k, z - 1, bottom, down))
 
     def z_second(k):
         return (z_send(4, k, z - 1, top, down), z_send(5, k, z + 1, bottom, up))
@@ -145,19 +176,18 @@
         for copy in copies:
             copy.start()
 
-    def own_operand():
-        for far in range(2):
-            for part in range(2):
-                k = far * 4 + part * 2 + c
-                at = ((y_lo + far) % 2) * 2 * LANES + part * LANES
-                rows = pl.ds(pl.multiple_of(at, LANES), LANES)
-                for s in range(2):
-                    w = w_ref[:, pl.ds(pl.multiple_of(y_lo * 2 * depth + s * depth, LANES), depth)]
-                    block = xs[s, 0, k].T * (w * scale)
-                    hi = block.astype(jnp.bfloat16)
-                    cols = pl.ds(s * depth, depth)
-                    ahi[rows, cols] = hi
-                    alo[rows, cols] = (block - hi.astype(jnp.float32)).astype(jnp.bfloat16)
+    def own_operand(far):
+        for part in range(2):
+            k = far * 4 + part * 2 + c
+            at = ((y_lo + far) % 2) * 2 * LANES + part * LANES
+            rows = pl.ds(pl.multiple_of(at, LANES), LANES)
+            for s in range(2):
+                w = w_ref[:, pl.ds(pl.multiple_of(y_lo * 2 * depth + s * depth, LANES), depth)]
+                block = xs[s, 0, k].T * (w * scale)
+                hi = block.astype(jnp.bfloat16)
+                cols = pl.ds(s * depth, depth)
+                ahi[rows, cols] = hi
+                alo[rows, cols] = (block - hi.astype(jnp.float32)).astype(jnp.bfloat16)
 
     def split(d, k, at):
         for s in range(2):
@@ -167,10 +197,29 @@
             bhi[rows, cols] = hi
             blo[rows, cols] = (block - hi.astype(jnp.float32)).astype(jnp.bfloat16)
 
-    def product():
+    def product(k, far):
         dot = functools.partial(jnp.dot, preferred_element_type=jnp.float32)
-        a, b = ahi[...], bhi[...]
-        return dot(a, b) + (dot(a, blo[...]) + dot(alo[...], b))
+        size = own // 2
+        rows = pl.ds(pl.multiple_of(((y_lo + far) % 2) * size, size), size)
+        a, b = ahi[rows, :], bhi[...]
+        out = dot(a, b) + (dot(a, blo[...]) + dot(alo[rows, :], b))
+        for d in range(4):
+            ps[k, d, rows] = out[:, d * LANES : (d + 1) * LANES]
+
+    def gathered(k):
+        for d in (1, 2, 3):
+            arrived(xs.at[1 - c, d, k], sem_s.at[d, k])
+        for d in range(4):
+            split(d, k, d * LANES)
+
+    def early(k):
+        gathered(k)
+        product(k, 0)
+        for b in range(2):
+
+            @pl.when(y_lo == b)
+            def _():
+                issue(z_first(k, b))
 
     def pass_on(k):
         arrived(xs.at[c, 3, k], sem_x.at[0, k])
@@ -183,33 +232,45 @@
         issue(last_share(k))
 
     def step(i, carry):
-        @pl.when(i < CHUNKS)
-        def _():
-            for d in (1, 2, 3):
-                arrived(xs.at[1 - c, d, i], sem_s.at[d, i])
+        @pl.when((i >= EARLY) & (i < CHUNKS))
+        def _():
+            gathered(i)
+            product(i, 0)
+
+        @pl.when(i < EARLY)
+        def _():
             for d in range(4):
                 split(d, i, d * LANES)
-            out = product()
-            for d in range(4):
-                ps[i, d] = out[:, d * LANES : (d + 1) * LANES]
-            issue(z_first(i))
-
-        @pl.when(i + 3 < CHUNKS)
-        def _():
-            pass_on(i + 3)
-
-        @pl.when(i + 5 < CHUNKS)
-        def _():
-            issue(first_hop(i + 5))
-
-        @pl.when(i + 3 == CHUNKS - 1)
-        def _():
-            for n in range(4, 16):
-                brick(n).start()
-
-        @pl.when(i + 2 < CHUNKS)
-        def _():
-            pass_last(i + 2)
+
+        @pl.when(i < CHUNKS)
+        def _():
+            product(i, 1)
+            for b in range(2):
+
+                @pl.when((i >= EARLY) | (y_lo != b))
+                def _():
+                    issue(z_first(i, b))
+
+        @pl.when((i >= 1) & (i + 2 < CHUNKS))
+        def _():
+            pass_on(i + 2)
+
+        @pl.when((i >= 1) & (i + 4 < CHUNKS))
+        def _():
+            issue(first_hop(i + 4))
+
+        @pl.when(i + 2 == CHUNKS - 1)
+        def _():
+            for dx, dc in over:
+                arrived(across.at[dx - 1, dc], sem_o.at[dx - 1, dc])
+            for n in range(4):
+                brick_far(n % 2, n // 2)[0].start()
+            for at in near:
+                brick_near(*at).start()
+
+        @pl.when((i >= 1) & (i + 1 < CHUNKS))
+        def _():
+            pass_last(i + 1)
 
         @pl.when((i >= 1) & (i < CHUNKS + 1))
         def _():
@@ -229,6 +290,13 @@
                 @pl.when(y != yr)
                 def _():
                     copy.start()
+
+        @pl.when(i == CHUNKS - 2)
+        def _():
+            for n in range(4):
+                g, dy = n // 2, n % 2
+                arrived(relay.at[g, dy], sem_r.at[g, dy])
+                brick_far(g, dy)[1].start()
 
         @pl.when(i >= 4 + LAG)
         def _():
@@ -251,6 +319,9 @@
         ready(k)
         if k < 2:
             issue(first_hop(k))
+    for k in range(4):
+        arrived(xs.at[1 - c, 0, k], sem_s.at[0, k])
+    own_operand(0)
     pass_on(0)
     issue(first_hop(2))
     pass_on(1)
@@ -258,39 +329,47 @@
     pass_last(0)
     ready(4)
     ready(5)
+    early(0)
     pass_on(2)
     issue(first_hop(4))
     pass_last(1)
     ready(6)
     ready(7)
+    early(1)
     brick(2).start()
     brick(3).start()
-    for k in range(CHUNKS):
+    for at in over:
+        brick_over(*at).start()
+    for k in range(4, CHUNKS):
         arrived(xs.at[1 - c, 0, k], sem_s.at[0, k])
-    own_operand()
+    own_operand(1)
     lax.fori_loop(0, CHUNKS + 1, step, 0)
     count = bricks.shape[0]
     for s in range(16):
         arrived(landed.at[pl.ds(s * count, count)], sem_b.at[s])
 
     def place(q, carry):
-        placed[q] = landed[order[0, q]]
+        tiles[q] = landed[order[0, q]]
         return carry
 
-    lax.fori_loop(0, placed.shape[0], place, 0)
-    written = pltpu.make_async_copy(placed, tiles, out_t)
-    written.start()
+    lax.fori_loop(0, tiles.shape[0], place, 0)
     lax.fori_loop(CHUNKS + 1, CHUNKS + LAG, step, 0)
-    written.wait()
 
     for part in range(2):
         for o in range(1, 4):
             reshard(o, part).wait_send()
-    for o in range(1, 16):
+    for o in (1, 2, 3):
         brick(o).wait_send()
+    for at in over:
+        brick_over(*at).wait_send()
+    for at in near:
+        brick_near(*at).wait_send()
+    for n in range(4):
+        for copy in brick_far(n // 2, n % 2):
+            copy.wait_send()
 
     def drain(k, carry):
-        for copy in (*first_hop(k), *first_share(k), *second_hop(k), *last_share(k), *z_first(k), *z_second(k)):
+        for copy in (*first_hop(k), *first_share(k), *second_hop(k), *last_share(k), *z_first(k, 0), *z_first(k, 1), *z_second(k)):
             copy.wait_send()
         for b in range(2):
             yr, copy = y_send(b, k)
@@ -315,11 +394,11 @@
     gram, tiles = pl.pallas_call(
         functools.partial(kernel, scale),
         out_shape=(
-            jax.ShapeDtypeStruct((2 * width, width), f32),
-            jax.ShapeDtypeStruct((count, BRICK, width), f32),
+            vmem((2 * width, width), f32),
+            vmem((count, BRICK, width), f32),
         ),
         in_specs=[space(pl.ANY), space(vmem), space(pl.ANY), space(pltpu.SMEM)],
-        out_specs=(space(vmem), space(pl.ANY)),
+        out_specs=(space(vmem), space(vmem)),
         scratch_shapes=[
             vmem((2, 4, CHUNKS, depth, LANES), f32),
             vmem((own, 2 * depth), bf16),
@@ -330,14 +409,15 @@
             vmem((6, CHUNKS, own // 2, LANES), f32),
             vmem((CHUNKS // 2, 3, own // 2, LANES), f32),
             vmem((count, BRICK, width), f32),
-            vmem((count, BRICK, width), f32),
+            vmem((2, 2, next_bricks.shape[0] // BRICK, BRICK, width), f32),
+            vmem((3, 2, next_bricks.shape[0] // BRICK, BRICK, width), f32),
             dma((CHUNKS,)), dma((2, CHUNKS)), dma((2, CHUNKS)), dma((4, CHUNKS)),
-            dma((6, CHUNKS)), dma((CHUNKS // 2, 3)), dma((16,)),
+            dma((6, CHUNKS)), dma((CHUNKS // 2, 3)), dma((16,)), dma((2, 2)), dma((3, 2)),
             dma((3, 2)), dma((2, CHUNKS)), dma((2, CHUNKS)), dma((4, CHUNKS)),
-            dma((6, CHUNKS)), dma((2, CHUNKS)), dma((15,)), dma,
+            dma((6, CHUNKS)), dma((2, CHUNKS)), dma((3,)), dma((2, 2, 2)), dma((3, 2)), dma((2, 2, 2)),
         ],
         compiler_params=pltpu.CompilerParams(
-            collective_id=0, has_side_effects=True, vmem_limit_bytes=60 * 1024 * 1024
+            collective_id=0, has_side_effects=True, vmem_limit_bytes=62464 * 1024
         ),
     )(snapshots, weights.reshape(1, rows), next_bricks.reshape(-1, BRICK, next_bricks.shape[1]), brick_source)
     return gram, tiles.reshape(rows, width)

time: 128 us -> 116 us (0.906)
  the two profiles are of different devices: /device:TPU:4 before, /device:TPU:6 now
where the time goes in v4:
time: 116 us; the launch traced here: 114 us
  Pallas kernels  111 us (96%)
  local copies, waits for them, and re-layouts  2.11 us (2%)
    pallas_call x1, Pallas kernels, per_device(): pl.pallas_call(functools.partial(kernel, scale), out_shape=(vmem((2 * wid...  111 us

profile of v4, /device:TPU:6, one launch (start us, length us, event | category | flops | bytes accessed | tf_op | source)
XLA Modules:
  0.0 114.1 jit_solution(17597051588303282886)
XLA Ops:
  0.6 111.4 %shard_map.59 = (f32[512,256]{1,0:T(8,128)S(1)}, f32[64,32,256]{2,1,0:T(8,128)S(1)}) custom-call(f32[2048,256]{1,0:T(8,128)} %snap.1, f32[1,2048]{1,0:T(1,128)} %bitcast.5, f32[4,32,4096]{2,1,0:T(8,128)} %bitcast.4, s32[1,64]{1,0:T(1,128)} %order.1), custom_call_target="tpu_custom_call" | custom-call | tf_op jit(solution)/shard_map/pallas_call | solution.py:394
  112.0 0.8 copy.8
  112.8 1.3 %copy.9 = f32[2048,256]{1,0:T(8,128)} copy(f32[2048,256]{1,0:T(8,128)S(1)} %bitcast.3) | data formatting | bytes 4194304

commit v5 on v4

v5 whole, which is shorter than its diff:
```python
import functools
import math

import jax
import jax.numpy as jnp
from jax import lax
from jax.experimental import pallas as pl
from jax.experimental.pallas import tpu as pltpu
from jax.sharding import PartitionSpec as P

BRICK = 32
NX, NZ = 4, 4
CHUNKS = 8
LANES = 128
LAG = 4
MESH = pl.DeviceIdType.MESH


def kernel(
    scale, snap, w_ref, bricks, gram, landed,
    xs, ahi, alo, bhi, blo, ps, zs, ys, relay, across, yin, vs,
    sem_a, sem_x, sem_h, sem_s, sem_z, sem_y, sem_b, sem_r, sem_o, sem_v, sem_w,
    sent,
):
    rb, me = lax.axis_index("rows"), lax.axis_index("snaps")
    z, y_hi = rb // 2, rb % 2
    x, y_lo, c = me // 4, (me // 2) % 2, me % 2
    y = y_hi * 2 + y_lo
    depth = xs.shape[3]
    half = depth // 2

    def snap_of(xx, yl, cc):
        return xx * 4 + yl * 2 + cc

    right = (rb, snap_of((x + 1) % NX, y_lo, c))
    left = (rb, snap_of((x + 3) % NX, y_lo, c))
    twin = (rb, snap_of(x, y_lo, 1 - c))
    up = (((z + 1) % NZ) * 2 + y_hi, me)
    down = (((z + 3) % NZ) * 2 + y_hi, me)

    def round_of(far, part, cc):
        if far == 0:
            return part * 3 + cc
        return 6 + cc if part else 2 + 3 * cc

    def send(src, dst, s_sem, r_sem, to):
        return pltpu.make_async_remote_copy(
            src_ref=src, dst_ref=dst, send_sem=s_sem, recv_sem=r_sem, device_id=to, device_id_type=MESH
        )

    def arrived(dst, sem):
        pltpu.make_async_copy(dst, dst, sem).wait()

    barrier = pltpu.get_barrier_semaphore()
    for o in range(1, 16):
        pl.semaphore_signal(barrier, inc=1, device_id=(rb, (me + o) % 16), device_id_type=MESH)
    pl.semaphore_signal(barrier, inc=1, device_id=up, device_id_type=MESH)
    pl.semaphore_signal(barrier, inc=1, device_id=down, device_id_type=MESH)
    for yl in range(2):
        far = (z * 2 + 1 - y_hi, snap_of(x, yl, c))
        pl.semaphore_signal(barrier, inc=1, device_id=far, device_id_type=MESH)
    pl.semaphore_wait(barrier, 19)

    def reshard(o, part):
        y2, c2 = (y_lo + o // 2) % 2, (c + o % 2) % 2
        q2 = y2 * 2 + c2
        k = round_of(o // 2, part, c)
        src = snap.at[pl.ds(pl.multiple_of(q2 * depth, depth), depth), pl.ds(part * LANES, LANES)]
        dst = xs.at[c2, 0, k]
        if o == 0:
            return pltpu.make_async_copy(src, dst, sem_a.at[k])
        to = (rb, snap_of(x, y2, c2))
        return send(src, dst, sent.at[0], sem_a.at[k], to)

    def brick(o):
        s2 = snap_of(x, (y_lo + o // 2) % 2, (c + o % 2) % 2)
        width = landed.shape[2]
        src = bricks.at[:, :, pl.ds(pl.multiple_of(s2 * width, LANES), width)]
        count = bricks.shape[0]
        dst = landed.at[pl.ds(me * count, count)]
        if o == 0:
            return pltpu.make_async_copy(src, dst, sem_b.at[0])
        return send(src, dst, sent.at[6], sem_b.at[0], (rb, s2))

    def brick_cols(dx, dy, dc):
        width = landed.shape[2]
        s2 = snap_of((x + dx) % NX, (y_lo + dy) % 2, (c + dc) % 2)
        return bricks.at[:, :, pl.ds(pl.multiple_of(s2 * width, LANES), width)]

    def rows_from(source):
        return landed.at[pl.ds(source * bricks.shape[0], bricks.shape[0])]

    def brick_over(dx, dc):
        to = (rb, snap_of(x, 1 - y_lo, c))
        dst = across.at[dx - 1, dc]
        return send(brick_cols(dx, 1, dc), dst, sent.at[6], sem_o.at[0], to)

    def held_bricks(dx, dy, dc):
        return across.at[dx - 1, dc] if dy else brick_cols(dx, 0, dc)

    def brick_near(dx, dy, dc):
        source = snap_of(x, (y_lo + dy) % 2, c)
        to = (rb, snap_of((x + dx) % NX, y_lo, (c + dc) % 2))
        sem = sent.at[7]
        return send(held_bricks(dx, dy, dc), rows_from(source), sem, sem_b.at[0], to)

    def brick_far(g, dy):
        ahead, behind = (x + 1 + 2 * g) % NX, (x + 3 - 2 * g) % NX
        source = snap_of(behind, (y_lo + dy) % 2, c)
        to = (rb, snap_of(ahead, y_lo, (c + g) % 2))
        hop = send(
            held_bricks(2, dy, g), relay.at[g, dy], sent.at[7], sem_r.at[g, dy], left if g else right
        )
        return hop, send(relay.at[g, dy], rows_from(source), sent.at[7], sem_b.at[0], to)

    near = [(dx, dy, dc) for dx in (1, 3) for dy in range(2) for dc in range(2)]
    over = [(dx, dc) for dx in (1, 2, 3) for dc in range(2)]

    for part in range(2):
        for o in (0, 1, 2, 3):
            reshard(o, part).start()
    brick(0).start()
    brick(1).start()

    def first_hop(k):
        return (
            send(xs.at[c, 0, k], xs.at[c, 3, k], sent.at[1], sem_x.at[0, k], right),
            send(xs.at[c, 0, k], xs.at[c, 1, k], sent.at[1], sem_x.at[1, k], left),
        )

    def first_share(k):
        return (send(xs.at[c, 0, k], xs.at[c, 0, k], sent.at[3], sem_s.at[0, k], twin),)

    def second_hop(k):
        lo_rows, hi_rows = pl.ds(0, half), pl.ds(half, half)
        return (
            send(xs.at[c, 3, k, lo_rows], xs.at[c, 2, k, lo_rows], sent.at[2], sem_h.at[k], right),
            send(xs.at[c, 1, k, hi_rows], xs.at[c, 2, k, hi_rows], sent.at[2], sem_h.at[k], left),
            send(xs.at[c, 3, k], xs.at[c, 3, k], sent.at[3], sem_s.at[3, k], twin),
            send(xs.at[c, 1, k], xs.at[c, 1, k], sent.at[3], sem_s.at[1, k], twin),
        )

    def last_share(k):
        return (send(xs.at[c, 2, k], xs.at[c, 2, k], sent.at[3], sem_s.at[2, k], twin),)

    own = ps.shape[2]
    top, bottom = pl.ds(0, own // 2), pl.ds(own // 2, own // 2)

    def slot_of(j):
        return (j - x + 2 * NX) % NX

    def z_send(n, k, j, rows, to):
        return send(ps.at[k, slot_of(j), rows], zs.at[n, k], sent.at[4], sem_z.at[min(n // 2, 1), k], to)

    def z_first(k, b):
        if b == 0:
            return (z_send(0, k, z + 2, top, down), z_send(2, k, z + 1, top, up))
        return (z_send(1, k, z + 2, bottom, up), z_send(3, k, z - 1, bottom, down))

    def z_second(k):
        return (z_send(4, k, z - 1, top, down), z_send(5, k, z + 1, bottom, up))

    def z_add(k, j, rows, ns):
        d = slot_of(j)
        total = ps[k, d, rows]
        for n in ns:
            total = total + zs[n, k]
        ps[k, d, rows] = total

    def y_send(b, k):
        far = k // 5
        h, m = (y_lo + far) % 2, (1 - far) * (k - k // 3) + far * (k - 4)
        yr = h * 2 + b
        slot = (y - yr + 8) % 4 - 1
        rows = top if b == 0 else bottom
        to = (z * 2 + h, snap_of(x, b, c))
        return yr, send(ps.at[k, slot_of(z), rows], ys.at[m, slot], sent.at[5], sem_y.at[m], to)

    def y_first(k, b):
        h = (y_lo + k // 2) % 2
        yr = h * 2 + b
        slot = (y - yr + 8) % 4 - 1
        rows = top if b == 0 else bottom
        to = (z * 2 + h, snap_of(x, b, c))
        return yr, send(ps.at[k, :, rows], yin.at[slot], sent.at[8], sem_v.at[0], to)

    def y_first_go(k):
        for b in range(2):
            yr, copy = y_first(k, b)

            @pl.when(y != yr)
            def _():
                copy.start()

    mine = ((y_hi + y_lo) % 2) * 2
    piece = own // 4

    def v_rows(part):
        return pl.ds(pl.multiple_of(y_lo * (own // 2) + part * piece, piece), piece)

    def v_send(n, j, part, to):
        return send(ps.at[mine, slot_of(j), v_rows(part)], vs.at[n], sent.at[9], sem_w.at[min(n // 2, 1)], to)

    def v_first():
        return (v_send(0, z + 2, 0, down), v_send(1, z + 2, 1, up), v_send(2, z + 1, 0, up), v_send(3, z - 1, 1, down))

    def v_second():
        return (v_send(4, z - 1, 0, down), v_send(5, z + 1, 1, up))

    def v_add(j, part, ns):
        d = slot_of(j)
        total = ps[mine, d, v_rows(part)]
        for n in ns:
            total = total + vs[n]
        ps[mine, d, v_rows(part)] = total

    def issue(copies):
        for copy in copies:
            copy.start()

    def own_operand(far):
        for part in range(2):
            k = round_of(far, part, c)
            at = ((y_lo + far) % 2) * 2 * LANES + part * LANES
            rows = pl.ds(pl.multiple_of(at, LANES), LANES)
            for s in range(2):
                w = w_ref[:, pl.ds(pl.multiple_of(y_lo * 2 * depth + s * depth, LANES), depth)]
                block = xs[s, 0, k].T * (w * scale)
                hi = block.astype(jnp.bfloat16)
                cols = pl.ds(s * depth, depth)
                ahi[rows, cols] = hi
                alo[rows, cols] = (block - hi.astype(jnp.float32)).astype(jnp.bfloat16)

    def split(d, k, at):
        for s in range(2):
            block = xs[s, d, k]
            hi = block.astype(jnp.bfloat16)
            rows, cols = pl.ds(s * depth, depth), pl.ds(at, LANES)
            bhi[rows, cols] = hi
            blo[rows, cols] = (block - hi.astype(jnp.float32)).astype(jnp.bfloat16)

    order_of = (0, 1, 3, 2)

    def product(far, k, k2, first=0, last=4):
        dot = functools.partial(jnp.dot, preferred_element_type=jnp.float32)
        size = own // 2
        rows = pl.ds(pl.multiple_of(((y_lo + far) % 2) * size, size), size)
        cols = pl.ds(first * LANES, (last - first) * LANES)
        a, b = ahi[rows, :], bhi[:, cols]
        out = dot(a, b) + (dot(a, blo[:, cols]) + dot(alo[rows, :], b))
        for n in range(first, last):
            d = order_of[n]
            ps[k2 if d == 2 else k, d, rows] = out[:, (n - first) * LANES : (n - first + 1) * LANES]

    def gathered(n, k):
        d = order_of[n]
        if d:
            arrived(xs.at[1 - c, d, k], sem_s.at[d, k])
        split(d, k, n * LANES)

    def z_go(k, late):
        for b in range(2):
            for j, copy in zip((z + 2, z + 1 - 2 * b), z_first(k, b)):

                @pl.when((slot_of(j) == 2) == late)
                def _():
                    copy.start()

    def early(k):
        for n in range(4):
            gathered(n, k)
        product(0, k, k)
        for b in range(2 if k else 0):

            @pl.when(y_lo == b)
            def _():
                issue(z_first(k, b))

    def pass_on(k):
        arrived(xs.at[c, 3, k], sem_x.at[0, k])
        arrived(xs.at[c, 1, k], sem_x.at[1, k])
        issue(second_hop(k))

    def pass_last(k):
        arrived(xs.at[c, 2, k], sem_h.at[k])
        issue(last_share(k))

    def step(i, carry):
        @pl.when(i + 1 < CHUNKS)
        def _():
            pass_on(i + 1)

        @pl.when(i + 3 < CHUNKS)
        def _():
            issue(first_hop(i + 3))

        @pl.when(i + 1 == CHUNKS - 1)
        def _():
            arrived(across, sem_o.at[0])
            for n in range(4):
                brick_far(n % 2, n // 2)[0].start()
            for at in near:
                brick_near(*at).start()

        @pl.when(i < CHUNKS)
        def _():
            pass_last(i)

        @pl.when(i + 1 < CHUNKS)
        def _():
            for n in range(3):
                gathered(n, i + 1)
            gathered(3, i)
            for far in range(2):
                product(far, i + 1, i)
            @pl.when(i == 2)
            def _():
                y_first_go(2)

            @pl.when(i > 2)
            def _():
                z_go(i, True)

            z_go(i + 1, False)

        @pl.when(i == CHUNKS - 1)
        def _():
            gathered(3, i)
            for far in range(2):
                product(far, i, i, first=3)
            z_go(i, True)

        def z_pass(k):
            arrived(zs.at[pl.ds(0, 2), k], sem_z.at[0, k])
            z_add(k, z - 1, top, (0,))
            z_add(k, z + 1, bottom, (1,))
            issue(z_second(k))

        def z_last(k):
            arrived(zs.at[pl.ds(2, 4), k], sem_z.at[1, k])
            z_add(k, z, top, (2, 4))
            z_add(k, z, bottom, (3, 5))
            for b in range(2):
                yr, copy = y_send(b, k)

                @pl.when(y != yr)
                def _():
                    copy.start()

        @pl.when((i != 3) & (i < CHUNKS + 1))
        def _():
            z_pass(i - 1)

        @pl.when((i == 4) | ((i >= 6) & (i < CHUNKS + 3)))
        def _():
            z_last(i - 3)

        @pl.when(i == CHUNKS - 1)
        def _():
            for n in range(4):
                g, dy = n // 2, n % 2
                arrived(relay.at[g, dy], sem_r.at[g, dy])
                brick_far(g, dy)[1].start()

        @pl.when(i == 7)
        def _():
            arrived(yin, sem_v.at[0])
            rows = pl.ds(pl.multiple_of(y_lo * (own // 2), own // 2), own // 2)
            for d in range(4):
                ps[mine, d, rows] = ps[mine, d, rows] + (yin[0, d] + (yin[1, d] + yin[2, d]))
            issue(v_first())

        @pl.when(i == 8)
        def _():
            arrived(vs.at[pl.ds(0, 2)], sem_w.at[0])
            v_add(z - 1, 0, (0,))
            v_add(z + 1, 1, (1,))
            issue(v_second())

        @pl.when(i == 10)
        def _():
            arrived(vs.at[pl.ds(2, 4)], sem_w.at[1])
            v_add(z, 0, (2, 4))
            v_add(z, 1, (3, 5))
            rows = pl.ds(pl.multiple_of(y_lo * (own // 2), own // 2), own // 2)
            gram[pl.ds(0, LANES), :] = ps[mine, slot_of(z), rows].T

        @pl.when(i >= 5 + LAG)
        def _():
            m = i - 4 - LAG
            far = (y_hi + y_lo) % 2
            k = (1 - far) * (m + m // 2) + far * (m + 4)
            arrived(ys.at[m], sem_y.at[m])
            here = ps[k, slot_of(z), pl.ds(pl.multiple_of(y_lo * (own // 2), own // 2), own // 2)]
            total = here + (ys[m, 0] + (ys[m, 1] + ys[m, 2]))
            at = (m % 2) * 2 * LANES + (m // 2) * LANES
            gram[pl.ds(pl.multiple_of(at, LANES), LANES), :] = total.T

        return carry

    def ready(k):
        arrived(xs.at[c, 0, k], sem_a.at[k])
        issue(first_share(k))

    for k in (0, 1, 3, 4):
        ready(k)
        if k < 2:
            issue(first_hop(k))
    for k in (0, 1, 3, 4):
        arrived(xs.at[1 - c, 0, k], sem_s.at[0, k])
    own_operand(0)
    pass_on(0)
    ready(2)
    issue(first_hop(2))
    pass_on(1)
    issue(first_hop(3))
    pass_last(0)
    ready(5)
    early(0)
    pass_on(2)
    issue(first_hop(4))
    pass_last(1)
    ready(6)
    ready(7)
    early(1)
    brick(2).start()
    brick(3).start()
    for at in over:
        brick_over(*at).start()
    for k in (2, 5, 6, 7):
        arrived(xs.at[1 - c, 0, k], sem_s.at[0, k])
    own_operand(1)
    for k in range(2):
        for n in range(4):
            split(order_of[n], k, n * LANES)
        product(1, k, k)
        if k == 0:
            y_first_go(0)
            continue
        for b in range(2):

            @pl.when(y_lo != b)
            def _():
                issue(z_first(k, b))

    for n in range(3):
        gathered(n, 2)
    for far in range(2):
        product(far, 2, 2, last=3)
    lax.fori_loop(2, CHUNKS + 3, step, 0)
    arrived(landed, sem_b.at[0])

    lax.fori_loop(CHUNKS + 3, CHUNKS + LAG, step, 0)

    all_sent = (
        xs.at[0, 0, pl.ds(0, 6)], xs.at[0, pl.ds(0, 2)], xs.at[0, 0], xs.at[0], zs.at[:, pl.ds(0, 6)],
        zs.at[pl.ds(0, 3), pl.ds(0, 3)], zs.at[pl.ds(0, 3), pl.ds(0, 3)], landed, yin, vs,
    )
    for n, ref in enumerate(all_sent):
        arrived(ref, sent.at[n])


def finish(order, gathered, summed, tiles, gram, sem_t, sem_g):
    for q in range(tiles.shape[0]):
        pltpu.make_async_copy(gathered.at[order[0, q]], tiles.at[q], sem_t).start()
    whole = pltpu.make_async_copy(summed, gram, sem_g)
    whole.start()
    pltpu.make_async_copy(gathered, tiles, sem_t).wait()
    whole.wait()


def per_device(snapshots, weights, next_bricks, brick_source):
    rows, width = snapshots.shape
    depth, own = rows // 4, 2 * width
    scale = 1.0 / math.sqrt(rows * lax.axis_size("rows"))
    f32, bf16, dma = jnp.float32, jnp.bfloat16, pltpu.SemaphoreType.DMA
    vmem = pltpu.VMEM
    space = lambda kind: pl.BlockSpec(memory_space=kind)
    count = rows // BRICK
    summed, landed = pl.pallas_call(
        functools.partial(kernel, scale),
        out_shape=(
            vmem((2 * width, width), f32),
            vmem((count, BRICK, width), f32),
        ),
        in_specs=[space(pl.ANY), space(vmem), space(pl.ANY)],
        out_specs=(space(vmem), space(pl.ANY)),
        scratch_shapes=[
            vmem((2, 4, CHUNKS, depth, LANES), f32),
            vmem((own, 2 * depth), bf16),
            vmem((own, 2 * depth), bf16),
            vmem((2 * depth, 4 * LANES), bf16),
            vmem((2 * depth, 4 * LANES), bf16),
            vmem((CHUNKS, 4, own, LANES), f32),
            vmem((6, CHUNKS, own // 2, LANES), f32),
            vmem((CHUNKS // 2, 3, own // 2, LANES), f32),
            vmem((2, 2, next_bricks.shape[0] // BRICK, BRICK, width), f32),
            vmem((3, 2, next_bricks.shape[0] // BRICK, BRICK, width), f32),
            vmem((3, 4, own // 2, LANES), f32),
            vmem((6, own // 4, LANES), f32),
            dma((CHUNKS,)), dma((2, CHUNKS)), dma((CHUNKS,)), dma((4, CHUNKS)), dma((2, CHUNKS)), dma((4,)),
            dma((1,)), dma((2, 2)), dma((1,)), dma((1,)), dma((2,)), dma((10,)),
        ],
        compiler_params=pltpu.CompilerParams(
            collective_id=0, has_side_effects=True, vmem_limit_bytes=62464 * 1024
        ),
    )(snapshots, weights.reshape(1, rows), next_bricks.reshape(-1, BRICK, next_bricks.shape[1]))
    tiles, gram = pl.pallas_call(
        finish,
        out_shape=(
            jax.ShapeDtypeStruct((count, BRICK, width), f32),
            jax.ShapeDtypeStruct((2 * width, width), f32),
        ),
        in_specs=[space(pltpu.SMEM), space(pl.ANY), space(pl.ANY)],
        out_specs=(space(pl.ANY), space(pl.ANY)),
        scratch_shapes=[dma, dma],
        compiler_params=pltpu.CompilerParams(vmem_limit_bytes=2 * 1024 * 1024),
    )(brick_source, landed, summed)
    return gram, tiles.reshape(rows, width)


def solution(mesh):
    return jax.shard_map(
        per_device,
        mesh=mesh,
        in_specs=(P("rows", "snaps"), P("rows"), P(("rows", "snaps"), None), P("rows", None)),
        out_specs=(P("rows", "snaps"), P("rows", "snaps")),
        check_vma=False,
    )
```

time: 116 us -> 110 us (0.948); the launches traced: 114 us -> 110 us
  local copies, waits for them, and re-layouts: 2.11 us -> 0.01 us
  Pallas kernels: 111 us -> 109 us
    pallas_call x1, Pallas kernels: 111 us -> 107 us  [per_device(): pl.pallas_call(functools.partial(kernel, scale), out_shape=(vmem((2 * wid...]
    unnamed x2, local copies, waits for them, and re-layouts: 2.11 us -> 0.01 us
    pallas_call x0 -> x1, Pallas kernels: none -> 2.03 us  [per_device(): pl.pallas_call(finish, out_shape=(jax.ShapeDtypeStruct((count, BRICK, wid...]
where the time goes in v5:
time: 110 us
  Pallas kernels  109 us (99%)
    pallas_call x1, Pallas kernels, per_device(): pl.pallas_call(functools.partial(kernel, scale), out_shape=(vmem((2 * wid...  107 us

profile of v5, /device:TPU:6, one launch (start us, length us, event | category | flops | bytes accessed | tf_op | source)
XLA Modules:
  0.0 109.6 jit_solution(12095125069514274425)
XLA Ops:
  0.6 0.0 copy-start
  0.6 106.9 %shard_map.59 = (f32[512,256]{1,0:T(8,128)S(1)}, f32[64,32,256]{2,1,0:T(8,128)S(1)}) custom-call(f32[2048,256]{1,0:T(8,128)} %snap.1, f32[1,2048]{1,0:T(1,128)} %bitcast.4, f32[4,32,4096]{2,1,0:T(8,128)} %bitcast.3), custom_call_target="tpu_custom_call" | custom-call | tf_op jit(solution)/shard_map/pallas_call | solution.py:480
  107.5 0.0 copy-done
  107.5 2.0 %shard_map.60 = (f32[64,32,256]{2,1,0:T(8,128)}, f32[512,256]{1,0:T(8,128)}) custom-call(s32[1,64]{1,0:T(1,128)S(1)} %copy-done, f32[64,32,256]{2,1,0:T(8,128)S(1)} %get-tuple-element.6.gathered, f32[512,256]{1,0:T(8,128)S(1)} %get-tuple-element.7.summed), custom_call_target="tpu_custom_call" | custom-call | tf_op jit(solution)/shard_map/pallas_call | solution.py:508
Async XLA Ops:
  0.6 106.9 %copy-start = (s32[1,64]{1,0:T(1,128)S(1)}, s32[1,64]{1,0:T(1,128)}, u32[]{:S(2)}) copy-start(s32[1,64]{1,0:T(1,128)} %order.1) | copy-start | bytes 772

commit v6 on v5

--- a/solution.py
+++ b/solution.py
@@ -40,7 +40,7 @@
 
     def round_of(far, part, cc):
         if far == 0:
-            return part * 3 + cc
+            return 3 + cc if part else 1 - cc
         return 6 + cc if part else 2 + 3 * cc
 
     def send(src, dst, s_sem, r_sem, to):
@@ -50,16 +50,6 @@
 
     def arrived(dst, sem):
         pltpu.make_async_copy(dst, dst, sem).wait()
-
-    barrier = pltpu.get_barrier_semaphore()
-    for o in range(1, 16):
-        pl.semaphore_signal(barrier, inc=1, device_id=(rb, (me + o) % 16), device_id_type=MESH)
-    pl.semaphore_signal(barrier, inc=1, device_id=up, device_id_type=MESH)
-    pl.semaphore_signal(barrier, inc=1, device_id=down, device_id_type=MESH)
-    for yl in range(2):
-        far = (z * 2 + 1 - y_hi, snap_of(x, yl, c))
-        pl.semaphore_signal(barrier, inc=1, device_id=far, device_id_type=MESH)
-    pl.semaphore_wait(barrier, 19)
 
     def reshard(o, part):
         y2, c2 = (y_lo + o // 2) % 2, (c + o % 2) % 2
@@ -117,9 +107,22 @@
     over = [(dx, dc) for dx in (1, 2, 3) for dc in range(2)]
 
     for part in range(2):
-        for o in (0, 1, 2, 3):
+        reshard(0, part).start()
+    brick(0).start()
+
+    barrier = pltpu.get_barrier_semaphore()
+    for o in range(1, 16):
+        pl.semaphore_signal(barrier, inc=1, device_id=(rb, (me + o) % 16), device_id_type=MESH)
+    pl.semaphore_signal(barrier, inc=1, device_id=up, device_id_type=MESH)
+    pl.semaphore_signal(barrier, inc=1, device_id=down, device_id_type=MESH)
+    for yl in range(2):
+        far = (z * 2 + 1 - y_hi, snap_of(x, yl, c))
+        pl.semaphore_signal(barrier, inc=1, device_id=far, device_id_type=MESH)
+    pl.semaphore_wait(barrier, 19)
+
+    for part in range(2):
+        for o in (1, 2, 3):
             reshard(o, part).start()
-    brick(0).start()
     brick(1).start()
 
     def first_hop(k):
@@ -169,7 +172,7 @@
 
     def y_send(b, k):
         far = k // 5
-        h, m = (y_lo + far) % 2, (1 - far) * (k - k // 3) + far * (k - 4)
+        h, m = (y_lo + far) % 2, (1 - far) * ((k + 2) // 2) + far * (k - 4)
         yr = h * 2 + b
         slot = (y - yr + 8) % 4 - 1
         rows = top if b == 0 else bottom
@@ -177,7 +180,7 @@
         return yr, send(ps.at[k, slot_of(z), rows], ys.at[m, slot], sent.at[5], sem_y.at[m], to)
 
     def y_first(k, b):
-        h = (y_lo + k // 2) % 2
+        h = (y_lo + k - 1) % 2
         yr = h * 2 + b
         slot = (y - yr + 8) % 4 - 1
         rows = top if b == 0 else bottom
@@ -192,7 +195,7 @@
             def _():
                 copy.start()
 
-    mine = ((y_hi + y_lo) % 2) * 2
+    mine = 1 + (y_hi + y_lo) % 2
     piece = own // 4
 
     def v_rows(part):
@@ -270,7 +273,7 @@
         for n in range(4):
             gathered(n, k)
         product(0, k, k)
-        for b in range(2 if k else 0):
+        for b in range(0 if k else 2):
 
             @pl.when(y_lo == b)
             def _():
@@ -347,22 +350,15 @@
                 def _():
                     copy.start()
 
-        @pl.when((i != 3) & (i < CHUNKS + 1))
+        @pl.when(i == 2)
+        def _():
+            z_pass(0)
+
+        @pl.when((i >= 4) & (i < CHUNKS + 1))
         def _():
             z_pass(i - 1)
 
-        @pl.when((i == 4) | ((i >= 6) & (i < CHUNKS + 3)))
-        def _():
-            z_last(i - 3)
-
-        @pl.when(i == CHUNKS - 1)
-        def _():
-            for n in range(4):
-                g, dy = n // 2, n % 2
-                arrived(relay.at[g, dy], sem_r.at[g, dy])
-                brick_far(g, dy)[1].start()
-
-        @pl.when(i == 7)
+        @pl.when(i == 8)
         def _():
             arrived(yin, sem_v.at[0])
             rows = pl.ds(pl.multiple_of(y_lo * (own // 2), own // 2), own // 2)
@@ -370,14 +366,29 @@
                 ps[mine, d, rows] = ps[mine, d, rows] + (yin[0, d] + (yin[1, d] + yin[2, d]))
             issue(v_first())
 
-        @pl.when(i == 8)
+        @pl.when(i == 4)
+        def _():
+            z_last(0)
+
+        @pl.when((i >= 6) & (i < CHUNKS + 3))
+        def _():
+            z_last(i - 3)
+
+        @pl.when(i == CHUNKS - 1)
+        def _():
+            for n in range(4):
+                g, dy = n // 2, n % 2
+                arrived(relay.at[g, dy], sem_r.at[g, dy])
+                brick_far(g, dy)[1].start()
+
+        @pl.when(i == 10)
         def _():
             arrived(vs.at[pl.ds(0, 2)], sem_w.at[0])
             v_add(z - 1, 0, (0,))
             v_add(z + 1, 1, (1,))
             issue(v_second())
 
-        @pl.when(i == 10)
+        @pl.when(i == 11)
         def _():
             arrived(vs.at[pl.ds(2, 4)], sem_w.at[1])
             v_add(z, 0, (2, 4))
@@ -389,7 +400,7 @@
         def _():
             m = i - 4 - LAG
             far = (y_hi + y_lo) % 2
-            k = (1 - far) * (m + m // 2) + far * (m + 4)
+            k = (1 - far) * (m + m // 2 - (3 - m) // 2) + far * (m + 4)
             arrived(ys.at[m], sem_y.at[m])
             here = ps[k, slot_of(z), pl.ds(pl.multiple_of(y_lo * (own // 2), own // 2), own // 2)]
             total = here + (ys[m, 0] + (ys[m, 1] + ys[m, 2]))
@@ -434,8 +445,8 @@
         for n in range(4):
             split(order_of[n], k, n * LANES)
         product(1, k, k)
-        if k == 0:
-            y_first_go(0)
+        if k == 1:
+            y_first_go(1)
             continue
         for b in range(2):
 

time: 110 us -> 106 us (0.964)
  Pallas kernels: 109 us -> 105 us
    pallas_call x1, Pallas kernels: 107 us -> 103 us  [per_device(): pl.pallas_call(functools.partial(kernel, scale), out_shape=(vmem((2 * wid...]
where the time goes in v6:
time: 106 us
  Pallas kernels  105 us (99%)
    pallas_call x1, Pallas kernels, per_device(): pl.pallas_call(functools.partial(kernel, scale), out_shape=(vmem((2 * wid...  103 us

profile of v6, /device:TPU:6, one launch (start us, length us, event | category | flops | bytes accessed | tf_op | source)
XLA Modules:
  0.0 105.9 jit_solution(15982115427198252668)
XLA Ops:
  0.6 0.0 copy-start
  0.6 103.2 %shard_map.59 = (f32[512,256]{1,0:T(8,128)S(1)}, f32[64,32,256]{2,1,0:T(8,128)S(1)}) custom-call(f32[2048,256]{1,0:T(8,128)} %snap.1, f32[1,2048]{1,0:T(1,128)} %bitcast.4, f32[4,32,4096]{2,1,0:T(8,128)} %bitcast.3), custom_call_target="tpu_custom_call" | custom-call | tf_op jit(solution)/shard_map/pallas_call | solution.py:491
  103.8 0.0 copy-done
  103.9 2.0 %shard_map.60 = (f32[64,32,256]{2,1,0:T(8,128)}, f32[512,256]{1,0:T(8,128)}) custom-call(s32[1,64]{1,0:T(1,128)S(1)} %copy-done, f32[64,32,256]{2,1,0:T(8,128)S(1)} %get-tuple-element.6.gathered, f32[512,256]{1,0:T(8,128)S(1)} %get-tuple-element.7.summed), custom_call_target="tpu_custom_call" | custom-call | tf_op jit(solution)/shard_map/pallas_call | solution.py:519
Async XLA Ops:
  0.6 103.2 %copy-start = (s32[1,64]{1,0:T(1,128)S(1)}, s32[1,64]{1,0:T(1,128)}, u32[]{:S(2)}) copy-start(s32[1,64]{1,0:T(1,128)} %order.1) | copy-start | bytes 772

commit v7 on v6

--- a/solution.py
+++ b/solution.py
@@ -17,9 +17,9 @@
 
 
 def kernel(
-    scale, snap, w_ref, bricks, gram, landed,
-    xs, ahi, alo, bhi, blo, ps, zs, ys, relay, across, yin, vs,
-    sem_a, sem_x, sem_h, sem_s, sem_z, sem_y, sem_b, sem_r, sem_o, sem_v, sem_w,
+    scale, snap, weights, bricks, gram, landed,
+    w_ref, xs, ahi, alo, bhi, blo, ps, zs, ys, relay, across, yin, vs,
+    sem_a, sem_x, sem_h, sem_s, sem_z, sem_y, sem_b, sem_r, sem_o, sem_v, sem_w, sem_c,
     sent,
 ):
     rb, me = lax.axis_index("rows"), lax.axis_index("snaps")
@@ -106,6 +106,8 @@
     near = [(dx, dy, dc) for dx in (1, 3) for dy in range(2) for dc in range(2)]
     over = [(dx, dc) for dx in (1, 2, 3) for dc in range(2)]
 
+    w_copy = pltpu.make_async_copy(weights, w_ref, sem_c)
+    w_copy.start()
     for part in range(2):
         reshard(0, part).start()
     brick(0).start()
@@ -261,13 +263,14 @@
             arrived(xs.at[1 - c, d, k], sem_s.at[d, k])
         split(d, k, n * LANES)
 
-    def z_go(k, late):
+    def z_go(k, late, direct):
         for b in range(2):
-            for j, copy in zip((z + 2, z + 1 - 2 * b), z_first(k, b)):
-
-                @pl.when((slot_of(j) == 2) == late)
-                def _():
-                    copy.start()
+            j = z + 1 - 2 * b if direct else z + 2
+            copy = z_first(k, b)[direct]
+
+            @pl.when((slot_of(j) == 2) == late)
+            def _():
+                copy.start()
 
     def early(k):
         for n in range(4):
@@ -308,6 +311,27 @@
         @pl.when(i < CHUNKS)
         def _():
             pass_last(i)
+
+        def z_pass(k):
+            arrived(zs.at[pl.ds(0, 2), k], sem_z.at[0, k])
+            z_add(k, z - 1, top, (0,))
+            z_add(k, z + 1, bottom, (1,))
+            issue(z_second(k))
+
+        def z_last(k):
+            arrived(zs.at[pl.ds(2, 4), k], sem_z.at[1, k])
+            z_add(k, z, top, (2, 4))
+            z_add(k, z, bottom, (3, 5))
+            for b in range(2):
+                yr, copy = y_send(b, k)
+
+                @pl.when(y != yr)
+                def _():
+                    copy.start()
+
+        @pl.when((i >= 4) & (i <= 6))
+        def _():
+            z_pass(i - 1)
 
         @pl.when(i + 1 < CHUNKS)
         def _():
@@ -322,39 +346,33 @@
 
             @pl.when(i > 2)
             def _():
-                z_go(i, True)
-
-            z_go(i + 1, False)
+                z_go(i, True, 0)
+
+            z_go(i + 1, False, 0)
+
+            @pl.when(i > 2)
+            def _():
+                z_go(i, True, 1)
+
+            @pl.when(i + 1 < CHUNKS - 1)
+            def _():
+                z_go(i + 1, False, 1)
 
         @pl.when(i == CHUNKS - 1)
         def _():
             gathered(3, i)
             for far in range(2):
                 product(far, i, i, first=3)
-            z_go(i, True)
-
-        def z_pass(k):
-            arrived(zs.at[pl.ds(0, 2), k], sem_z.at[0, k])
-            z_add(k, z - 1, top, (0,))
-            z_add(k, z + 1, bottom, (1,))
-            issue(z_second(k))
-
-        def z_last(k):
-            arrived(zs.at[pl.ds(2, 4), k], sem_z.at[1, k])
-            z_add(k, z, top, (2, 4))
-            z_add(k, z, bottom, (3, 5))
+            z_go(i, True, 0)
+            z_pass(i - 1)
             for b in range(2):
-                yr, copy = y_send(b, k)
-
-                @pl.when(y != yr)
-                def _():
-                    copy.start()
+                z_first(i, b)[1].start()
 
         @pl.when(i == 2)
         def _():
             z_pass(0)
 
-        @pl.when((i >= 4) & (i < CHUNKS + 1))
+        @pl.when(i == CHUNKS)
         def _():
             z_pass(i - 1)
 
@@ -419,6 +437,7 @@
             issue(first_hop(k))
     for k in (0, 1, 3, 4):
         arrived(xs.at[1 - c, 0, k], sem_s.at[0, k])
+    w_copy.wait()
     own_operand(0)
     pass_on(0)
     ready(2)
@@ -494,9 +513,10 @@
             vmem((2 * width, width), f32),
             vmem((count, BRICK, width), f32),
         ),
-        in_specs=[space(pl.ANY), space(vmem), space(pl.ANY)],
+        in_specs=[space(pl.ANY), space(pl.ANY), space(pl.ANY)],
         out_specs=(space(vmem), space(pl.ANY)),
         scratch_shapes=[
+            vmem((1, rows), f32),
             vmem((2, 4, CHUNKS, depth, LANES), f32),
             vmem((own, 2 * depth), bf16),
             vmem((own, 2 * depth), bf16),
@@ -510,7 +530,7 @@
             vmem((3, 4, own // 2, LANES), f32),
             vmem((6, own // 4, LANES), f32),
             dma((CHUNKS,)), dma((2, CHUNKS)), dma((CHUNKS,)), dma((4, CHUNKS)), dma((2, CHUNKS)), dma((4,)),
-            dma((1,)), dma((2, 2)), dma((1,)), dma((1,)), dma((2,)), dma((10,)),
+            dma((1,)), dma((2, 2)), dma((1,)), dma((1,)), dma((2,)), dma, dma((10,)),
         ],
         compiler_params=pltpu.CompilerParams(
             collective_id=0, has_side_effects=True, vmem_limit_bytes=62464 * 1024

time: 106 us -> 103 us (0.972)
  Pallas kernels: 105 us -> 101 us
    pallas_call x1, Pallas kernels: 103 us -> 99.3 us  [per_device(): pl.pallas_call(functools.partial(kernel, scale), out_shape=(vmem((2 * wid...]
where the time goes in v7:
time: 103 us; the launch traced here: 102 us
  Pallas kernels  101 us (98%)
    pallas_call x1, Pallas kernels, per_device(): pl.pallas_call(functools.partial(kernel, scale), out_shape=(vmem((2 * wid...  99.3 us

profile of v7, /device:TPU:6, one launch (start us, length us, event | category | flops | bytes accessed | tf_op | source)
XLA Modules:
  0.0 102.0 jit_solution(12809963477834574133)
XLA Ops:
  0.6 0.0 copy-start
  0.6 99.3 %shard_map.59 = (f32[512,256]{1,0:T(8,128)S(1)}, f32[64,32,256]{2,1,0:T(8,128)S(1)}) custom-call(f32[2048,256]{1,0:T(8,128)} %snap.1, f32[1,2048]{1,0:T(1,128)} %bitcast.4, f32[4,32,4096]{2,1,0:T(8,128)} %bitcast.3), custom_call_target="tpu_custom_call" | custom-call | tf_op jit(solution)/shard_map/pallas_call | solution.py:510
  100.0 0.0 copy-done
  100.0 2.0 %shard_map.60 = (f32[64,32,256]{2,1,0:T(8,128)}, f32[512,256]{1,0:T(8,128)}) custom-call(s32[1,64]{1,0:T(1,128)S(1)} %copy-done, f32[64,32,256]{2,1,0:T(8,128)S(1)} %get-tuple-element.6.gathered, f32[512,256]{1,0:T(8,128)S(1)} %get-tuple-element.7.summed), custom_call_target="tpu_custom_call" | custom-call | tf_op jit(solution)/shard_map/pallas_call | solution.py:539
Async XLA Ops:
  0.6 99.3 %copy-start = (s32[1,64]{1,0:T(1,128)S(1)}, s32[1,64]{1,0:T(1,128)}, u32[]{:S(2)}) copy-start(s32[1,64]{1,0:T(1,128)} %order.1) | copy-start | bytes 772

commit v8 on v7

--- a/solution.py
+++ b/solution.py
@@ -129,8 +129,8 @@
 
     def first_hop(k):
         return (
-            send(xs.at[c, 0, k], xs.at[c, 3, k], sent.at[1], sem_x.at[0, k], right),
-            send(xs.at[c, 0, k], xs.at[c, 1, k], sent.at[1], sem_x.at[1, k], left),
+            send(xs.at[c, 0, k], xs.at[c, 3, k], sent.at[1], sem_x.at[k], right),
+            send(xs.at[c, 0, k], xs.at[c, 1, k], sent.at[1], sem_x.at[k], left),
         )
 
     def first_share(k):
@@ -283,8 +283,7 @@
                 issue(z_first(k, b))
 
     def pass_on(k):
-        arrived(xs.at[c, 3, k], sem_x.at[0, k])
-        arrived(xs.at[c, 1, k], sem_x.at[1, k])
+        arrived(xs.at[c, pl.ds(0, 2), k], sem_x.at[k])
         issue(second_hop(k))
 
     def pass_last(k):
@@ -491,10 +490,10 @@
 
 
 def finish(order, gathered, summed, tiles, gram, sem_t, sem_g):
+    whole = pltpu.make_async_copy(summed, gram, sem_g)
+    whole.start()
     for q in range(tiles.shape[0]):
         pltpu.make_async_copy(gathered.at[order[0, q]], tiles.at[q], sem_t).start()
-    whole = pltpu.make_async_copy(summed, gram, sem_g)
-    whole.start()
     pltpu.make_async_copy(gathered, tiles, sem_t).wait()
     whole.wait()
 
@@ -529,7 +528,7 @@
             vmem((3, 2, next_bricks.shape[0] // BRICK, BRICK, width), f32),
             vmem((3, 4, own // 2, LANES), f32),
             vmem((6, own // 4, LANES), f32),
-            dma((CHUNKS,)), dma((2, CHUNKS)), dma((CHUNKS,)), dma((4, CHUNKS)), dma((2, CHUNKS)), dma((4,)),
+            dma((CHUNKS,)), dma((CHUNKS,)), dma((CHUNKS,)), dma((4, CHUNKS)), dma((2, CHUNKS)), dma((4,)),
             dma((1,)), dma((2, 2)), dma((1,)), dma((1,)), dma((2,)), dma, dma((10,)),
         ],
         compiler_params=pltpu.CompilerParams(

time: 103 us -> 102 us (level)
  no operation moved by 1% of the time
where the time goes in v8:
time: 102 us
  Pallas kernels  101 us (99%)
    pallas_call x1, Pallas kernels, per_device(): pl.pallas_call(functools.partial(kernel, scale), out_shape=(vmem((2 * wid...  99.3 us

profile of v8, /device:TPU:6, one launch (start us, length us, event | category | flops | bytes accessed | tf_op | source)
XLA Modules:
  0.0 101.9 jit_solution(13719643007799639687)
XLA Ops:
  0.6 0.0 copy-start
  0.6 99.3 %shard_map.59 = (f32[512,256]{1,0:T(8,128)S(1)}, f32[64,32,256]{2,1,0:T(8,128)S(1)}) custom-call(f32[2048,256]{1,0:T(8,128)} %snap.1, f32[1,2048]{1,0:T(1,128)} %bitcast.4, f32[4,32,4096]{2,1,0:T(8,128)} %bitcast.3), custom_call_target="tpu_custom_call" | custom-call | tf_op jit(solution)/shard_map/pallas_call | solution.py:509
  99.9 0.0 copy-done
  99.9 2.0 %shard_map.60 = (f32[64,32,256]{2,1,0:T(8,128)}, f32[512,256]{1,0:T(8,128)}) custom-call(s32[1,64]{1,0:T(1,128)S(1)} %copy-done, f32[64,32,256]{2,1,0:T(8,128)S(1)} %get-tuple-element.6.gathered, f32[512,256]{1,0:T(8,128)S(1)} %get-tuple-element.7.summed), custom_call_target="tpu_custom_call" | custom-call | tf_op jit(solution)/shard_map/pallas_call | solution.py:538
Async XLA Ops:
  0.6 99.3 %copy-start = (s32[1,64]{1,0:T(1,128)S(1)}, s32[1,64]{1,0:T(1,128)}, u32[]{:S(2)}) copy-start(s32[1,64]{1,0:T(1,128)} %order.1) | copy-start | bytes 772
